TPU v7x, 256 devices: a whole 4x4x8 slice. The times are simulated.
256 devices in a mesh: dp: 32 (over z, y), tp: 8 (over x, core).
Axes of the slice: x: 4, y: 4, z: 8, core: 2. Of those that a mesh axis runs over, the one named last changes fastest.
Arguments:
- embed_table: bfloat16 [50304, 2048], P('tp')
- tok_ids: int32 [32, 512], P('dp')
- tok_labels: int32 [32, 512], P('dp')
- trunk_out: bfloat16 [32, 512, 2048], P('dp')
Outputs:
- output 1: float32 [], replicated
- output 2: bfloat16 [32, 512, 2048], P('dp')
- output 3: float32 [50304, 2048], P('tp')
All inputs are finite; a program needn't handle non-finite values.
Results may differ from a plain program's by a relative error of at most 0.001.
Values sent between devices are 32-bit elements.
A program may use at most 768 MiB of HBM per device.

v0:
```python
import jax
import jax.numpy as jnp
from jax import lax
from jax.sharding import PartitionSpec as P

LN_EPS = 1e-5


def layer_norm(hidden):
    mean_h = jnp.mean(hidden, axis=-1, keepdims=True)
    centered = hidden - mean_h
    inv_std = lax.rsqrt(jnp.mean(centered * centered, axis=-1, keepdims=True) + LN_EPS)
    return centered * inv_std, inv_std


def norm_backward(grad_normed, normed, inv_std):
    mean_g = jnp.mean(grad_normed, axis=-1, keepdims=True)
    mean_gu = jnp.mean(grad_normed * normed, axis=-1, keepdims=True)
    return inv_std * (grad_normed - mean_g - normed * mean_gu)


def solution(mesh):
    dp_size = mesh.shape['dp']

    def per_device(table_loc, ids_loc, labels_loc, trunk_loc):
        shard_rows, model_width = table_loc.shape
        batch_loc, seq_len = ids_loc.shape
        tok_local = batch_loc * seq_len
        tok_total = tok_local * dp_size
        row_start = lax.axis_index('tp') * shard_rows
        local_ids = ids_loc.reshape(tok_local) - row_start
        own_ids = jnp.where((local_ids >= 0) & (local_ids < shard_rows), local_ids, shard_rows)
        partial_emb = jnp.take(table_loc, own_ids, axis=0, mode='fill', fill_value=0).astype(jnp.float32)
        embedded = lax.psum(partial_emb, 'tp')
        hidden = embedded + trunk_loc.reshape(tok_local, model_width).astype(jnp.float32)
        normed, inv_std = layer_norm(hidden)
        normed_bf = normed.astype(jnp.bfloat16)
        logits = lax.dot_general(normed_bf, table_loc, (((1,), (1,)), ((), ())), preferred_element_type=jnp.float32)
        row_max = lax.pmax(jnp.max(logits, axis=-1, keepdims=True), 'tp')
        shifted = jnp.exp(logits - row_max)
        sum_exp = lax.psum(jnp.sum(shifted, axis=-1, keepdims=True), 'tp')
        local_labels = labels_loc.reshape(tok_local) - row_start
        is_label = jnp.arange(shard_rows)[None, :] == local_labels[:, None]
        label_logit = lax.psum(jnp.sum(jnp.where(is_label, logits, 0.0), axis=-1), 'tp')
        tok_loss = jnp.log(sum_exp[:, 0]) + row_max[:, 0] - label_logit
        mean_loss = lax.psum(jnp.sum(tok_loss), 'dp') / tok_total
        grad_logits = ((shifted / sum_exp - is_label.astype(jnp.float32)) / tok_total).astype(jnp.bfloat16)
        grad_normed = lax.psum(jnp.dot(grad_logits, table_loc, preferred_element_type=jnp.float32), 'tp')
        grad_hidden = norm_backward(grad_normed, normed, inv_std)
        head_grad = lax.dot_general(grad_logits, normed_bf, (((0,), (0,)), ((), ())), preferred_element_type=jnp.float32)
        table_grad = head_grad.at[own_ids].add(grad_hidden, mode='drop')
        table_grad = lax.psum(table_grad, 'dp')
        d_trunk = grad_hidden.astype(jnp.bfloat16).reshape(batch_loc, seq_len, model_width)
        return mean_loss, d_trunk, table_grad

    return jax.shard_map(per_device, mesh=mesh, in_specs=(P('tp', None), P('dp', None), P('dp', None), P('dp', None, None)), out_specs=(P(), P('dp', None, None), P('tp', None)), check_vma=False)
```

profile of v0, /device:TPU:1, one launch (start us, length us, event | category | flops | bytes accessed | tf_op | source)
XLA Modules:
  0.0 1187.1 jit_solution(4625212970505887074)
XLA Ops:
  7.2 0.7 compare_select_fusion
  7.9 16.9 %gather_fusion = bf16[512,2048]{1,0:T(8,128)(2,1)} fusion(bf16[6288,2048]{1,0:T(8,128)(2,1)} %param.4, s32[1024]{0:T(1024)S(1)} %pad_clamp_fusion), kind=kCustom, calls=%fused_computation | custom fusion | bytes 4196352 | tf_op jit(solution)/shard_map/jit(_take)/gather | solution.py:33
  24.8 4.1 select_convert_fusion
  29.2 79.1 %all-reduce.5.cloned.1.call-done = f32[512,2048]{1,0:T(8,128)} async-done(((f32[512,2048]{1,0:T(8,128)}), f32[512,2048]{1,0:T(8,128)}) %all-reduce.5.cloned.1.call-update) | async-done | bytes 4194320 | tf_op jit(solution)/shard_map/psum | solution.py:34
  108.3 2.8 fusion.2
  111.2 0.6 copy-done
  111.8 0.8 multiply_reduce_fusion.1
  112.6 0.7 fusion.1
  113.4 20.6 %fusion.6 = (f32[512]{0:T(512)S(1)}, f32[512,6288]{0,1:T(8,128)}) fusion(bf16[512,2048]{1,0:T(8,128)(2,1)S(1)} %fusion.1, bf16[6288,2048]{1,0:T(8,128)(2,1)} %param.4), kind=kOutput, calls=%fused_computation.31 | convolution fusion | flops 13190111232 | bytes 40732672 | tf_op jit(solution)/shard_map/dot_general | solution.py:38
  134.0 14.3 %pmax.7 = f32[512]{0:T(512)S(1)} all-reduce(f32[512]{0:T(512)S(1)} %get-tuple-element.13), channel_id=1, replica_groups=mesh['dp'=32,'tp'=8] {'tp'}, use_global_device_ids=true, to_apply=%region_4.5 | all-reduce | flops 512 | bytes 4096 | tf_op jit(solution)/shard_map/pmax | solution.py:39
  148.3 6.8 fusion
  155.1 14.2 %all-reduce = (f32[512]{0:T(512)S(1)}, f32[512]{0:T(512)S(1)}) all-reduce(f32[512]{0:T(512)S(1)} %get-tuple-element.4, f32[512]{0:T(512)S(1)} %get-tuple-element.3), channel_id=1, replica_groups=mesh['dp'=32,'tp'=8] {'tp'}, use_global_device_ids=true, to_apply=%region_8.9 | all-reduce | flops 1024 | bytes 8192 | tf_op jit(solution)/shard_map/psum | solution.py:44
  169.4 24.0 %fusion.4 = f32[512,2048]{1,0:T(8,128)} fusion(bf16[6288,2048]{1,0:T(8,128)(2,1)} %param.4, f32[512,6288]{0,1:T(8,128)} %get-tuple-element.14, f32[512]{0:T(512)S(1)} %get-tuple-element.8, s32[512]{0:T(512)S(1)} %bitcast.29, f32[512]{0:T(512)S(1)} %pmax.7), kind=kOutput, calls=%fused_computation.29 | convolution fusion | flops 13209427968 | bytes 42833920 | tf_op jit(solution)/shard_map/dot_general | solution.py:48
  193.4 0.3 all-reduce.9.cloned.1.call-start
  193.7 26.3 %fusion.3 = f32[6288,2048]{1,0:T(8,128)} fusion(bf16[512,2048]{1,0:T(8,128)(2,1)} %copy-done.4, f32[512,6288]{0,1:T(8,128)} %get-tuple-element.14, f32[512]{0:T(512)S(1)} %get-tuple-element.8, s32[512]{0:T(512)S(1)} %bitcast.30, f32[512]{0:T(512)S(1)} %pmax.7), kind=kOutput, calls=%fused_computation.28 | convolution fusion | flops 13209427968 | bytes 66492416 | tf_op jit(solution)/shard_map/dot_general | solution.py:50
  220.0 47.9 %all-reduce.7.cloned.1.call-done = f32[512,2048]{1,0:T(8,128)} async-done(((f32[512,2048]{1,0:T(8,128)}), f32[512,2048]{1,0:T(8,128)}) %all-reduce.7.cloned.1.call-update) | async-done | bytes 4194320 | tf_op jit(solution)/shard_map/psum | solution.py:48
  267.9 4.7 fusion.5
  272.6 1.2 copy-done.3
  273.8 3.6 convert_bitcast_fusion
  277.4 41.7 %scatter_fusion = f32[6288,2048]{1,0:T(8,128)} fusion(f32[6288,2048]{1,0:T(8,128)} %fusion.3, s32[512]{0:T(512)S(1)} %bitcast.26, f32[512,2048]{1,0:T(8,128)} %get-tuple-element.10), kind=kCustom, calls=%fused_computation.1 | custom fusion | flops 1048576 | bytes 12584960 | tf_op jit(solution)/shard_map/scatter-add | solution.py:51
  319.1 0.6 subtract_reduce_fusion
  319.7 62.8 %psum.45 = f32[]{:T(128)} all-reduce(f32[]{:T(128)} %subtract_reduce_fusion), channel_id=1, replica_groups=mesh['dp'=32,'tp'=8] {'dp'}, use_global_device_ids=true, to_apply=%region_10.11 | all-reduce | flops 1 | bytes 8 | tf_op jit(solution)/shard_map/psum | solution.py:46
  383.1 760.6 %all-reduce.9.cloned.1.call-done = f32[6288,2048]{1,0:T(8,128)} async-done(((f32[6288,2048]{1,0:T(8,128)}), f32[6288,2048]{1,0:T(8,128)}) %all-reduce.9.cloned.1.call-update) | async-done | bytes 51511312 | tf_op jit(solution)/shard_map/psum | solution.py:52
  1143.7 35.7 %copy.11 = f32[6288,2048]{1,0:T(8,128)} copy(f32[6288,2048]{1,0:T(8,128)} %all-reduce.9.cloned.1.call-done) | data formatting | bytes 103022592
  (21 shorter events, 0.4 us)
Async XLA Ops:
  7.2 101.2 %all-reduce.5.cloned.1.call-start = ((), (), s32[]{:S(2)}) async-start(), calls=%async_computation | async-start | bytes 8388608 | tf_op jit(solution)/shard_map/psum | solution.py:34
  24.8 4.4 copy-start.5
  24.8 83.5 %copy-start.2 = (bf16[1,512,2048]{2,1,0:T(8,128)(2,1)S(1)}, bf16[1,512,2048]{2,1,0:T(8,128)(2,1)}, u32[]{:S(2)}) copy-start(bf16[1,512,2048]{2,1,0:T(8,128)(2,1)} %param.7) | copy-start | bytes 6291460
  28.9 238.9 %all-reduce.7.cloned.1.call-start = ((), (), s32[]{:S(2)}) async-start(), calls=%async_computation.1 | async-start | bytes 8388608 | tf_op jit(solution)/shard_map/psum | solution.py:48
  108.3 3.4 copy-start
  113.3 20.6 %copy-start.4 = (bf16[512,2048]{1,0:T(8,128)(2,1)}, bf16[512,2048]{1,0:T(8,128)(2,1)S(1)}, u32[]{:S(2)}) copy-start(bf16[512,2048]{1,0:T(8,128)(2,1)S(1)} %fusion.1) | copy-start | bytes 6291460
  193.4 950.3 %all-reduce.9.cloned.1.call-start = ((), (), s32[]{:S(2)}) async-start(), calls=%async_computation.2 | async-start | bytes 103022592 | tf_op jit(solution)/shard_map/psum | solution.py:52
  267.9 4.7 copy-start.1
  267.9 5.9 copy-start.3
Sparse Core Ops, SparseCore 0:
  29.1 79.2 all-reduce.4
  193.5 74.3 all-reduce.6
  319.2 824.4 all-reduce.8
where the time goes:
time: 1190 us
  waiting for transfers between devices  888 us (75%)
  blocking collectives  91.3 us (8%)
  matrix products  70.9 us (6%)
  other arithmetic  66.6 us (6%)
  local copies, waits for them, and re-layouts  54.4 us (5%)
  between operations  15.6 us (1%)
    psum x1, waiting for transfers between devices, per_device(): table_grad = lax.psum(table_grad, 'dp')  761 us
    psum x1, waiting for transfers between devices, per_device(): embedded = lax.psum(partial_emb, 'tp')  79.1 us
    psum x1, blocking collectives, per_device(): mean_loss = lax.psum(jnp.sum(tok_loss), 'dp') / tok_total  62.8 us
    psum x1, waiting for transfers between devices, per_device(): lax.psum(jnp.dot(grad_logits, table_loc, preferred_element_type=jnp.float...  47.9 us
    scatter-add x1, other arithmetic, per_device(): table_grad = head_grad.at[own_ids].add(grad_hidden, mode='drop')  41.7 us
    unnamed x13, local copies, waits for them, and re-layouts  37.5 us
    dot_general x1, matrix products, per_device(): lax.dot_general(grad_logits, normed_bf, (((0,), (0,)), ((), ())), preferr...  26.3 us
    dot_general x1, matrix products, per_device(): jnp.dot(grad_logits, table_loc, preferred_element_type=jnp.float32)  24 us
  transfers between devices with their start and end apart: 3, of which 3 were waited for; matrix products, arithmetic and copies ran while one was open for 2% of the time, Pallas kernels for 0%

commit v1 on v0

v1 whole, which is shorter than its diff:
```python
import functools
import heapq

import jax
import jax.numpy as jnp
from jax import lax
from jax.experimental import pallas as pl
from jax.experimental.pallas import tpu as pltpu
from jax.sharding import PartitionSpec as P

LN_EPS = 1e-5
MESH = pl.DeviceIdType.MESH
F32, BF16 = jnp.float32, jnp.bfloat16
NY, NTP, NX = 4, 8, 4
WAYS = (1, -1)
ALL = Ellipsis
NEG = float(jnp.finfo(jnp.float32).min)
VT = 512
NT_DIMS = (((1,), (1,)), ((), ()))
NN_DIMS = (((1,), (0,)), ((), ()))


def rem(a, b):
    return lax.rem(a, jnp.int32(b))


class Place:
    def __init__(self, nz):
        self.nz = nz
        self.dp = lax.axis_index("dp")
        self.tp = lax.axis_index("tp")
        self.z, self.y = lax.div(self.dp, jnp.int32(NY)), rem(self.dp, NY)
        self.x, self.c = lax.div(self.tp, jnp.int32(2)), rem(self.tp, 2)
        self.partner = 2 * self.x + (1 - self.c)

    def tp_of(self, step, other=False):
        c = 1 - self.c if other else self.c
        return 2 * rem(self.x + step + NX, NX) + c

    def y_of(self, step):
        return rem(self.y + step + NY, NY)

    def dp_of_y(self, step):
        return self.z * NY + self.y_of(step)

    def dp_of_z(self, step):
        return rem(self.z + step + self.nz, self.nz) * NY + self.y


def to_tp(tp):
    return {"tp": tp}


def to_dp(dp):
    return {"dp": dp}


def rdma(src, dst, send_sem, recv_sem, device):
    return pltpu.make_async_remote_copy(
        src_ref=src, dst_ref=dst, send_sem=send_sem, recv_sem=recv_sem, device_id=device, device_id_type=MESH
    )


def greet(devices):
    barrier = pltpu.get_barrier_semaphore()
    for device in devices:
        pl.semaphore_signal(barrier, inc=1, device_id=device, device_id_type=MESH)
    pl.semaphore_wait(barrier, len(devices))


def reduce_scatter_tp(at, src, own, pb, rl, fin, send, recv, meanwhile=lambda: None):
    half = own // 2
    pair = []
    for i, step in enumerate((2, 1, -1, 0)):
        row = pl.multiple_of(at.tp_of(step, True) * own, own)
        pair.append(rdma(src.at[pl.ds(row, own)], pb.at[i], send.at[i], recv.at[i], to_tp(at.partner)))
        pair[-1].start()
    rows = [pl.multiple_of(at.tp_of(step) * own, own) for step in (2, 1, -1, 0)]
    plus, minus = to_tp(at.tp_of(1)), to_tp(at.tp_of(-1))

    def merge(i):
        pair[i].wait_recv()
        pb[i] = pb[i] + src[pl.ds(rows[i], own), :]

    def half_of(i, h):
        return pb.at[i, pl.ds(h * half, half)]

    merge(0)
    far = [
        rdma(half_of(0, 0), rl.at[0], send.at[4], recv.at[4], plus),
        rdma(half_of(0, 1), rl.at[1], send.at[5], recv.at[5], minus),
    ]
    for copy in far:
        copy.start()
    merge(1)
    merge(2)
    near = [
        rdma(half_of(1, 1), fin.at[0], send.at[6], recv.at[6], plus),
        rdma(half_of(2, 0), fin.at[1], send.at[7], recv.at[7], minus),
        rdma(half_of(1, 0), fin.at[2], send.at[8], recv.at[8], plus),
        rdma(half_of(2, 1), fin.at[3], send.at[9], recv.at[9], minus),
    ]
    near[0].start()
    near[1].start()
    far[0].wait_recv()
    pb[1, pl.ds(0, half)] = pb[1, pl.ds(0, half)] + rl[0]
    near[2].start()
    far[1].wait_recv()
    pb[2, pl.ds(half, half)] = pb[2, pl.ds(half, half)] + rl[1]
    near[3].start()
    merge(3)
    meanwhile()
    for copy in near:
        copy.wait_recv()
    top = pb[3, pl.ds(0, half)] + fin[2] + fin[1]
    low = pb[3, pl.ds(half, half)] + fin[0] + fin[3]
    for copy in pair + far + near:
        copy.wait_send()
    return jnp.concatenate([top, low], axis=0)


def gather_plan(sizes, parts, latency, busy=(), hold=0):
    sends, events, heap, busy = [], [], [], dict(busy)

    def post(axis, way, off, lo, hi, order, now):
        end = max(now, busy.get((axis, way), now)) + hi - lo
        busy[axis, way] = end
        there = tuple(o - way * (a == axis) for a, o in enumerate(off))
        heapq.heappush(heap, (end + latency, len(sends), there, lo, hi, order))
        sends.append((axis, way, off, lo, hi))
        return len(sends) - 1

    def ring(axis, way, off, lo, hi, order, now):
        last = sizes[axis] // 2
        gone = abs(off[axis]) + 1
        if gone > last or lo == hi:
            return []
        if gone == last:
            mid = lo + 8 * pl.cdiv(hi - lo, 16)
            lo, hi = (lo, mid) if way > 0 else (mid, hi)
        return [post(axis, way, off, lo, hi, order, now)]

    starts = [[] for _ in parts]
    for leg in range(2):
        for begin, (lo, hi, order, now) in zip(starts, parts):
            for way in WAYS:
                begin += ring(order[leg], way, (0, 0), lo, hi, order, now)
    while heap:
        now, i, off, lo, hi, order = heapq.heappop(heap)
        axis, way = sends[i][:2]
        if off[1] and now < hold:
            heapq.heappush(heap, (hold, i, off, lo, hi, order))
            continue
        new = ring(axis, way, off, lo, hi, order, now)
        if axis == order[0]:
            for w in WAYS:
                new += ring(order[1], w, off, lo, hi, order, now)
        events.append((i, new, now))
    return sends, starts, events


def two_colours(lo, hi, share, now=0):
    split = lo + 8 * round((hi - lo) * share / 8)
    return [(lo, split, (0, 1), now), (split, hi, (1, 0), now)]


class Spread:
    def __init__(self, at, plan, rows, block, send, recv):
        self.sends, self.starts, self.events = plan
        self.block, self.send, self.recv, self.rows = block, send, recv, rows
        self.count = len(self.sends)
        self.other = to_tp(at.partner)
        self.device = {}
        for way in WAYS:
            self.device[0, way] = to_tp(at.tp_of(way))
            self.device[1, way] = to_dp(at.dp_of_y(way))

    def goal(self, i):
        axis, way, off = self.sends[i][:3]
        return tuple(o - way * (a == axis) for a, o in enumerate(off))

    def copy(self, i):
        axis, way, off, lo, hi = self.sends[i]
        src, dst = self.block(*off, False, lo, hi), self.block(off[0], self.goal(i)[1], False, lo, hi)
        return rdma(src, dst, self.send.at[i], self.recv.at[i], self.device[axis, way])

    def forward(self, i, cross=False):
        off, (lo, hi) = ((0, 0), (0, self.rows)) if i == self.count else (self.goal(i), self.sends[i][-2:])
        ref = self.block(*off, cross, lo, hi)
        return rdma(ref, ref, self.send.at[self.count + i], self.recv.at[self.count + i], self.other)

    def begin(self):
        for i in sum(self.starts, []):
            self.copy(i).start()
        self.forward(self.count).start()

    def run(self, events):
        for i, new, _ in events:
            ref = self.block(*self.goal(i), False, *self.sends[i][-2:])
            rdma(ref, ref, self.send.at[i], self.recv.at[i], self.other).wait_recv()
            for j in new:
                self.copy(j).start()
            self.forward(i).start()

    def take(self, i):
        self.forward(i, True).wait_recv()

    def end(self):
        for i in range(self.count):
            self.copy(i).wait_send()
        for i in range(self.count + 1):
            self.forward(i).wait_send()


def token_kernel(
    nz, tok_total, plan, table, part, trunk, lab_col, lab_row, ids,
    du, ub_out, ub_far, u_out, r_out, stats, tiles,
    table_v, ub_v, z_v, run, mine, theirs, row_out, row_in, tile_out, tile_in, pb, rl, fin, land,
    load_sem, part_sem, st_send, st_recv, row_send, row_recv, t_send, t_recv, rs_send, rs_recv, x_send, x_recv,
):
    at = Place(nz)
    rows, width = table_v.shape
    toks = ub_v.shape[0]
    own = trunk.shape[0]
    steps = z_v.shape[0]
    whole = rows // VT
    tail = rows - whole * VT

    part_copy = pltpu.make_async_copy(part, du, part_sem)
    part_copy.start()

    def load(i):
        start = pl.multiple_of(i * VT, 16)
        return pltpu.make_async_copy(table.at[pl.ds(start, VT)], table_v.at[pl.ds(start, VT)], load_sem.at[i])

    tail_copy = pltpu.make_async_copy(
        table.at[pl.ds(whole * VT, tail)], table_v.at[pl.ds(whole * VT, tail)], load_sem.at[whole]
    )
    greet([to_tp(rem(at.tp + i, NTP)) for i in range(1, NTP)] + [to_dp(at.dp_of_y(i)) for i in range(1, NY)])
    part_copy.wait()
    for i in range(whole):
        load(i).start()
    tail_copy.start()
    hidden = reduce_scatter_tp(at, du, own, pb, rl, fin, rs_send, rs_recv) + trunk[ALL].astype(F32)
    centered = hidden - jnp.mean(hidden, axis=-1, keepdims=True)
    inv_std = lax.rsqrt(jnp.mean(centered * centered, axis=-1, keepdims=True) + LN_EPS)
    normed = centered * inv_std
    land[at.tp] = normed.astype(BF16).astype(F32)

    def block(dx, dy, cross, lo, hi):
        tp, cut = at.tp_of(dx, cross), pl.ds(lo, hi - lo)
        return ub_far.at[dy % NY - 1, tp, cut] if dy % NY else land.at[tp, cut]

    spread = Spread(at, plan, own, block, x_send, x_recv)
    spread.begin()
    u_out[ALL] = normed
    r_out[ALL] = jnp.broadcast_to(inv_std, r_out.shape)
    near = [e for e in spread.events if spread.goal(e[0])[1] == 0]
    spread.run(near)
    for e in near:
        spread.take(e[0])
    spread.take(spread.count)
    groups = {}
    pace = own / 7.5
    for e in [e for e in spread.events if e not in near]:
        due = max(0, int((e[-1] - near[-1][-1]) / pace)) + 2
        groups.setdefault(due if due <= steps else max(steps, due - 5), []).append(e)
    late = [e for due in sorted(groups) if due >= 2 * steps for e in groups[due]]

    def attend(step):
        for due, events in groups.items():
            if due < 2 * steps:

                @pl.when(step == due)
                def _(events=events):
                    spread.run(events)

    keep = pltpu.make_async_copy(land, ub_out, part_sem)
    keep.start()
    ub_v[ALL] = land[ALL].reshape(toks, width).astype(BF16)
    run[0] = jnp.full(run.shape[1:], NEG, F32)
    run[1] = jnp.zeros(run.shape[1:], F32)
    lane = lax.broadcasted_iota(jnp.int32, (toks, VT), 1)

    def start_of(i):
        return pl.multiple_of(jnp.minimum(i * VT, rows - VT), 16)

    def fold(op, v):
        return functools.reduce(op, [v[:, j : j + 128] for j in range(0, VT, 128)])

    def forward(i, carry):
        attend(i)

        @pl.when(i < whole)
        def _():
            load(i).wait()

        @pl.when(i == whole)
        def _():
            tail_copy.wait()

        start = start_of(i)
        z = lax.dot_general(ub_v[ALL], table_v[pl.ds(start, VT), :], NT_DIMS, preferred_element_type=F32)
        z = jnp.where(lane >= i * VT - start, z, NEG)
        z_v[i] = z
        run[0] = jnp.maximum(run[0], fold(jnp.maximum, z))
        hit = (lane + start == lab_col[ALL]) & (lane >= i * VT - start)
        run[1] = run[1] + fold(jnp.add, jnp.where(hit, z, 0.0))
        return carry

    lax.fori_loop(0, steps, forward, 0)
    top = jnp.max(run[0], axis=1, keepdims=True)
    run[0] = jnp.zeros(run.shape[1:], F32)

    def exps(i, carry):
        run[0] = run[0] + fold(jnp.add, jnp.exp(z_v[i] - top))
        return carry

    lax.fori_loop(0, steps, exps, 0)
    sums = jnp.sum(run[0], axis=1, keepdims=True)
    label = jnp.sum(run[1], axis=1, keepdims=True)
    narrow = lax.broadcasted_iota(jnp.int32, (toks, 128), 1)
    packed = jnp.where(narrow == 0, top, jnp.where(narrow == 1, sums, jnp.where(narrow == 2, label, 0.0)))
    mine[ALL] = jnp.transpose(packed)[:8]
    stat = []
    for i in range(1, NTP):
        stat.append(rdma(mine, theirs.at[i], st_send.at[i], st_recv.at[i], to_tp(rem(at.tp + i, NTP))))
        stat[-1].start()
    theirs[0] = mine[ALL]
    for copy in stat:
        copy.wait_recv()
    parts = [theirs[rem(at.tp - j + NTP, NTP)] for j in range(NTP)]
    peak = functools.reduce(jnp.maximum, [p[0:1] for p in parts])
    total = functools.reduce(jnp.add, [p[1:2] * jnp.exp(p[0:1] - peak) for p in parts])
    label = functools.reduce(jnp.add, [p[2:3] for p in parts])
    lse = peak + jnp.log(total)
    loss = jnp.sum(jnp.log(total) + peak - label, axis=1, keepdims=True)
    sub = lax.broadcasted_iota(jnp.int32, (8, toks), 0)
    row_out[ALL] = jnp.where(sub == 0, lse, jnp.where(sub == 1, lab_row[ALL], 0.0))
    tiles[0, 0:8] = ids[ALL]
    tiles[0, 8:16] = jnp.broadcast_to(loss, ids.shape)
    tile_out[ALL] = tiles[0]
    rows_sent = []
    for i in range(NY - 1):
        to_y = to_dp(at.dp_of_y(NY - 1 - i))
        rows_sent.append(rdma(row_out, row_in.at[i], row_send.at[i], row_recv.at[i], to_y))
        rows_sent.append(rdma(tile_out, tile_in.at[i], t_send.at[i], t_recv.at[i], to_y))
    for copy in rows_sent:
        copy.start()
    run[0] = jnp.transpose(jnp.broadcast_to(lse, (128, toks)))
    wide = min(512, width)
    inv_total = 1.0 / tok_total
    du[ALL] = jnp.zeros(du.shape, F32)

    def backward(i, carry):
        attend(i + steps)
        start = start_of(i)
        shift = jnp.concatenate([run[0]] * (VT // 128), axis=1)
        prob = jnp.exp(z_v[i] - shift)
        hit = (lane + start == lab_col[ALL]) & (lane >= i * VT - start)
        grad = ((prob - jnp.where(hit, 1.0, 0.0)) * inv_total).astype(BF16)
        for n in range(width // wide):
            cols = pl.ds(n * wide, wide)
            du[:, cols] = du[:, cols] + lax.dot_general(
                grad, table_v[pl.ds(start, VT), cols], NN_DIMS, preferred_element_type=F32
            )
        return carry

    lax.fori_loop(0, steps, backward, 0)
    spread.run(late)
    for e in spread.events:
        if e not in near:
            spread.take(e[0])
    for copy in rows_sent:
        copy.wait_recv()
    stats[0] = row_out[ALL]
    for i in range(NY - 1):
        stats[i + 1] = row_in[i]
        tiles[i + 1] = tile_in[i]
    keep.wait()
    spread.end()
    for copy in stat + rows_sent:
        copy.wait_send()


def head_kernel(nz, stride, tok_total, table, ub, ub_far, stats, out, table_v, ub_v, stage, grad_v, load_sem, stage_sem):
    step = pl.program_id(0)
    dp, tp = lax.axis_index("dp"), lax.axis_index("tp")
    win, width = table_v.shape
    tile = out.shape[1]
    toks = stage.shape[1]
    first = pl.multiple_of(rem(dp, NY) * stride, 16)

    @pl.when(step == 0)
    def _():
        load = pltpu.make_async_copy(table.at[pl.ds(first, win)], table_v, load_sem)
        load.start()
        copies = [pltpu.make_async_copy(ub, stage.at[0], stage_sem.at[0])]
        for i in range(1, NY):
            copies.append(pltpu.make_async_copy(ub_far.at[i - 1], stage.at[i % 2], stage_sem.at[i % 2]))
        copies[0].start()
        copies[1].start()
        for i in range(NY):
            copies[i].wait()
            ub_v[pl.ds(i * toks, toks)] = stage[i % 2].astype(BF16)
            if i + 2 < NY:
                copies[i + 2].start()
        load.wait()

    begin = pl.multiple_of(step * tile, 16)
    vocab = tp * table.shape[0] + first + begin + lax.broadcasted_iota(jnp.int32, (tile, toks), 0)
    inv_total = 1.0 / tok_total

    def logits(n, carry):
        at_tok = pl.multiple_of(n * toks, 128)
        z = lax.dot_general(
            table_v[pl.ds(begin, tile), :], ub_v[pl.ds(at_tok, toks), :], NT_DIMS, preferred_element_type=F32
        )
        row = stats[n]
        prob = jnp.exp(z - row[0:1])
        hit = vocab == row[1:2].astype(jnp.int32)
        grad_v[:, pl.ds(at_tok, toks)] = ((prob - jnp.where(hit, 1.0, 0.0)) * inv_total).astype(BF16)
        return carry

    lax.fori_loop(0, NY, logits, 0)
    cols = out.shape[2]

    def sums(n, carry):
        at_col = pl.multiple_of(n * cols, 128)
        out[n] = jnp.dot(grad_v[ALL], ub_v[:, pl.ds(at_col, cols)], preferred_element_type=F32)
        return carry

    lax.fori_loop(0, nz, sums, 0)


class SumZ:
    def __init__(self, at, source, parts, came, total, chunks, send, recv):
        self.at, self.source, self.parts, self.came, self.total = at, source, parts, came, total
        self.chunks, self.send, self.recv = chunks, send, recv
        self.last = at.nz // 2

    def rows(self, c, s, way):
        lo, hi = self.chunks[c]
        if s == 1:
            mid = lo + 8 * pl.cdiv(hi - lo, 16)
            lo, hi = (lo, mid) if way > 0 else (mid, hi)
        return pl.ds(lo, hi - lo)

    def goal(self, s, way):
        return rem(self.at.z + way * (self.last + 1 - s) + self.at.nz, self.at.nz)

    def copy(self, c, s, way):
        rows, w = self.rows(c, s, way), WAYS.index(way)
        src = (self.source if s == 1 else self.parts).at[self.goal(s, way), rows]
        sems = self.send.at[w, s, c], self.recv.at[w, s, c]
        return rdma(src, self.came.at[w, s - 1, rows], *sems, to_dp(self.at.dp_of_z(way)))

    def begin(self):
        for c in range(len(self.chunks)):
            for way in WAYS:
                self.copy(c, 1, way).start()

    def run(self, c, s):
        for w, way in enumerate(WAYS):
            self.copy(c, s, way).wait_recv()
            rows = self.rows(c, s, way)
            if s < self.last:
                goal = self.goal(s + 1, way)
                self.parts[goal, rows] = self.parts[goal, rows] + self.came[w, s - 1, rows]
                self.copy(c, s + 1, way).start()
            else:
                self.total[rows] = self.total[rows] + self.came[w, s - 1, rows]

    def end(self):
        for c in range(len(self.chunks)):
            for s in range(self.last):
                for way in WAYS:
                    self.copy(c, s + 1, way).wait_send()


def finish_kernel(
    nz, stride, vocab_loc, row_plan, dh_plan, table_plan, chunks, du, u, r, tiles, head,
    d_trunk, loss, stack,
    pb, rl, fin, land, all_dh, all_tiles, parts, came, total,
    rs_send, rs_recv, row_send, row_recv, z_send, z_recv, i_send, i_recv, x_send, x_recv, s_send, s_recv, t_send, t_recv,
    load_sem,
):
    at = Place(nz)
    own, width = u.shape
    cols = width // nz
    block = nz * own
    load = pltpu.make_async_copy(head, parts, load_sem)
    load.start()
    greet(
        [to_tp(rem(at.tp + i, NTP)) for i in range(1, NTP)]
        + [to_dp(at.dp_of_z(i)) for i in range(1, nz)]
        + [to_dp(at.dp_of_y(way)) for way in WAYS]
    )
    sums = SumZ(at, head, parts, came, total, chunks, s_send, s_recv)
    sums.begin()
    todo = [(c, s) for s in range(1, sums.last + 1) for c in range(len(chunks))]

    def first_sum():
        load.wait()
        total[ALL] = parts[at.z]
        sums.run(*todo[0])

    grad = reduce_scatter_tp(at, du, own, pb, rl, fin, rs_send, rs_recv, first_sum)
    normed = u[ALL]
    mean_g = jnp.mean(grad, axis=-1, keepdims=True)
    mean_gu = jnp.mean(grad * normed, axis=-1, keepdims=True)
    land[at.tp] = r[:, 0:1] * (grad - mean_g - normed * mean_gu)

    def row_block(dx, dy, cross, lo, hi):
        return land.at[at.tp_of(dx, cross), pl.ds(lo, hi - lo)]

    whole_rows = Spread(at, row_plan, own, row_block, row_send, row_recv)
    whole_rows.begin()
    here = pl.multiple_of(at.z * own, own)
    turned = []
    for i in range(1, nz):
        col, to_z = pl.multiple_of(rem(at.z + i, nz) * cols, 128), to_dp(at.dp_of_z(i))
        turned.append(
            rdma(
                land.at[at.tp, :, pl.ds(col, cols)], all_dh.at[at.tp, 0, pl.ds(here, own)],
                z_send.at[i], z_recv.at[i], to_z,
            )
        )
        turned.append(rdma(tiles, all_tiles.at[at.z], i_send.at[i], i_recv.at[i], to_z))
    for copy in turned:
        copy.start()
    my_col = pl.multiple_of(at.z * cols, 128)
    all_dh[at.tp, 0, pl.ds(here, own)] = land[at.tp, :, pl.ds(my_col, cols)]
    all_tiles[at.z] = tiles[ALL]
    for c, s in todo[1 : len(chunks)]:
        sums.run(c, s)
    whole_rows.run(whole_rows.events)
    for copy in turned:
        copy.wait_recv()

    def dh_block(dx, dy, cross, lo, hi):
        return all_dh.at[at.tp_of(dx, cross), dy % NY, pl.ds(lo, hi - lo)]

    blocks = Spread(at, dh_plan, block, dh_block, x_send, x_recv)
    blocks.begin()
    for i in range(whole_rows.count + 1):
        whole_rows.take(i)
    d_trunk[ALL] = land[ALL].reshape(d_trunk.shape).astype(BF16)
    loss[ALL] = sum(
        all_tiles[z, rem(y - at.y + NY, NY), 8:16] for z in range(nz) for y in range(NY)
    )

    pieces = {(0, 0): [(blocks.count, [], 0)]}
    for e in blocks.events:
        dx, dy = blocks.goal(e[0])
        pieces.setdefault((dx % NX, dy % NY), []).append(e)
    order = sorted((pieces[p][-1][-1] + cross * (block // 3), *p, cross) for p in pieces for cross in range(2))
    left = list(blocks.events)
    due = []
    for time, dx, dy, cross in order:
        due.append([e for e in left if e[-1] <= time])
        left = [e for e in left if e[-1] > time]
    code = [dx + NX * (dy + NY * cross) for _, dx, dy, cross in order]
    beside = {k * len(order) // 3: todo[len(chunks) + k] for k in range(min(3, len(todo) - len(chunks)))}

    win = total.shape[0]
    tile = win // 3 if win % 48 == 0 else win
    low = (at.tp * vocab_loc + at.y * stride).astype(F32)

    def piece(e, carry):
        mark = jnp.int32(code[0])
        for k in range(len(order)):
            mark = jnp.where(e == k, code[k], mark)
            _, dx, dy, cross = order[k]
            if due[k] or cross or k in beside:

                @pl.when(e == k)
                def _(k=k, dx=dx, dy=dy, cross=cross):
                    if k in beside:
                        sums.run(*beside[k])
                    blocks.run(due[k])
                    if cross:
                        for part in pieces[dx, dy]:
                            blocks.take(part[0])

        core = jnp.where(mark >= NX * NY, 1 - at.c, at.c)
        tp = 2 * rem(at.x + rem(mark, NX), NX) + core
        far = rem(lax.div(mark, jnp.int32(NX)), NY)
        ids = jnp.concatenate(
            [
                all_tiles[2 * j, far, pl.ds(tp, 1), :] + all_tiles[2 * j + 1, far, pl.ds(tp, 1), :]
                for j in range(nz // 2)
            ],
            axis=1,
        )
        dh = all_dh[tp, far]
        hi = dh.astype(BF16)
        rest = dh - hi.astype(F32)
        mid = rest.astype(BF16)
        lo = (rest - mid.astype(F32)).astype(BF16)
        ids = (ids - low).astype(jnp.int32)
        for begin in range(0, win, tile):
            row = lax.broadcasted_iota(jnp.int32, (tile, block), 0) + begin
            pick = jnp.where(row == ids, 1.0, 0.0).astype(BF16)
            found = sum(jnp.dot(pick, term, preferred_element_type=F32) for term in (hi, mid, lo))
            total[begin : begin + tile] = total[begin : begin + tile] + found
        return carry

    lax.fori_loop(0, len(order), piece, 0)
    for copy in turned:
        copy.wait_send()

    sends, starts, events = table_plan
    device = {(0, way): to_dp(at.dp_of_z(way)) for way in WAYS} | {(1, way): to_dp(at.dp_of_y(way)) for way in WAYS}

    def copy_of(i, arrives=False):
        axis, way, off, lo, hi = sends[i]
        if arrives:
            off = tuple(o - way * (a == axis) for a, o in enumerate(off))
        dst = stack.at[rem(at.z + off[0] + nz, nz), at.y_of(off[1]), pl.ds(lo, hi - lo)]
        src = dst if any(off) else total.at[pl.ds(lo, hi - lo)]
        return rdma(src, dst, t_send.at[i], t_recv.at[i], device[axis, way])

    keeps = []
    after = todo[len(chunks) + len(beside) :]
    for c, (lo, hi) in enumerate(chunks):
        while (c, sums.last) in after:
            sums.run(*after.pop(0))
        for i in sum(starts[2 * c : 2 * c + 2], []):
            copy_of(i).start()
        rows = pl.ds(lo, hi - lo)
        keeps.append(pltpu.make_async_copy(total.at[rows], stack.at[at.z, at.y, rows], load_sem))
    for i, new, _ in events:
        copy_of(i, True).wait_recv()
        for j in new:
            copy_of(j).start()
    for keep in keeps:
        keep.start()
        keep.wait()
    for i in range(len(sends)):
        copy_of(i).wait_send()
    sums.end()
    whole_rows.end()
    blocks.end()


def place_kernel(chunk, stack, out, slots, load_sem, store_sem):
    nz, ny, have, cols = stack.shape
    depth = slots.shape[0]
    per = have // chunk
    total = ny * per
    ahead = depth // 2

    def load(i):
        y, row = lax.div(i, jnp.int32(per)), pl.multiple_of(rem(i, per) * chunk, 8)
        s = rem(i, depth)
        return pltpu.make_async_copy(stack.at[:, y, pl.ds(row, chunk)], slots.at[s], load_sem.at[s])

    def stores(i):
        s, row = rem(i, depth), pl.multiple_of(i * chunk, 8)
        return [
            pltpu.make_async_copy(slots.at[s, j], out.at[pl.ds(row, chunk), pl.ds(j * cols, cols)], store_sem.at[s, j])
            for j in range(nz)
        ]

    def prime(i, carry):
        load(i).start()
        return carry

    def body(i, carry):
        load(i).wait()
        for copy in stores(i):
            copy.start()

        @pl.when(i + ahead < total)
        def _():
            @pl.when(i >= ahead)
            def _():
                for copy in stores(i - ahead):
                    copy.wait()

            load(i + ahead).start()

        return carry

    def drain(i, carry):
        for copy in stores(i):
            copy.wait()
        return carry

    lax.fori_loop(0, ahead, prime, 0)
    lax.fori_loop(0, total, body, 0)
    lax.fori_loop(total - 2 * ahead, total, drain, 0)
    used = per * chunk
    left = have - used
    rest = pltpu.make_async_copy(stack.at[:, ny - 1, pl.ds(used, left)], slots.at[0, :, pl.ds(0, left)], load_sem.at[0])
    rest.start()
    rest.wait()
    tails = [
        pltpu.make_async_copy(
            slots.at[0, j, pl.ds(0, left)], out.at[pl.ds(ny * used, left), pl.ds(j * cols, cols)], store_sem.at[0, j]
        )
        for j in range(nz)
    ]
    for copy in tails:
        copy.start()
    for copy in tails:
        copy.wait()


def vmem():
    return pl.BlockSpec(memory_space=pltpu.VMEM)


def anywhere():
    return pl.BlockSpec(memory_space=pl.ANY)


def dma(*shape):
    return pltpu.SemaphoreType.DMA(shape)


def solution(mesh):
    ndp, ntp = mesh.shape["dp"], mesh.shape["tp"]
    nz = ndp // NY

    def per_device(table, ids, labels, trunk):
        vocab_loc, width = table.shape
        batch, seq = ids.shape
        toks = batch * seq
        own = toks // NTP
        tok_total = toks * ndp
        stride = (vocab_loc - 16) // NY
        win = stride + 16
        cols = width // nz
        block = nz * own
        big = 66_000_000
        dp, tp = lax.axis_index("dp"), lax.axis_index("tp")
        row_start = tp * vocab_loc
        local_ids = ids.reshape(toks) - row_start
        own_ids = jnp.where((local_ids >= 0) & (local_ids < vocab_loc), local_ids, vocab_loc)
        part = jnp.take(table, own_ids, axis=0, mode="fill", fill_value=0).astype(F32)
        trunk_own = lax.dynamic_slice_in_dim(trunk.reshape(toks, width), tp * own, own, 0)

        tp_scratch = [
            pltpu.VMEM((4, own, width), F32),
            pltpu.VMEM((2, own // 2, width), F32),
            pltpu.VMEM((4, own // 2, width), F32),
            pltpu.VMEM((NTP, own, width), F32),
        ]
        ids_f = ids.reshape(NTP, own).astype(F32)
        blank = jnp.zeros_like(ids_f)
        even = rem(lax.div(dp, jnp.int32(NY)), 2) == 0
        pad = ((0, 0), (0, 128 - 2 * own))
        ids_tile = jnp.pad(jnp.concatenate([jnp.where(even, ids_f, blank), jnp.where(even, blank, ids_f)], axis=1), pad)
        lab_col = labels.reshape(toks, 1) - row_start
        lab_row = labels.reshape(1, toks).astype(F32)
        steps = pl.cdiv(vocab_loc, VT)
        token_plan = gather_plan((NX, NY), two_colours(0, own, 0.5), 16, hold=2 * own)
        sends = 2 * len(token_plan[0]) + 1
        du, ub, ub_far, u_own, r_own, stats, tiles = pl.pallas_call(
            functools.partial(token_kernel, nz, tok_total, token_plan),
            out_shape=(
                jax.ShapeDtypeStruct((toks, width), F32),
                jax.ShapeDtypeStruct((NTP, own, width), F32),
                jax.ShapeDtypeStruct((NY - 1, NTP, own, width), F32),
                jax.ShapeDtypeStruct((own, width), F32),
                jax.ShapeDtypeStruct((own, 128), F32),
                jax.ShapeDtypeStruct((NY, 8, toks), F32),
                jax.ShapeDtypeStruct((NY, 16, 128), F32),
            ),
            in_specs=[anywhere(), anywhere(), vmem(), vmem(), vmem(), vmem()],
            out_specs=(vmem(), anywhere(), anywhere(), vmem(), vmem(), vmem(), vmem()),
            scratch_shapes=[
                pltpu.VMEM((vocab_loc, width), BF16),
                pltpu.VMEM((toks, width), BF16),
                pltpu.VMEM((steps, toks, VT), F32),
                pltpu.VMEM((2, toks, 128), F32),
                pltpu.VMEM((8, toks), F32),
                pltpu.VMEM((NTP, 8, toks), F32),
                pltpu.VMEM((8, toks), F32),
                pltpu.VMEM((NY - 1, 8, toks), F32),
                pltpu.VMEM((16, 128), F32),
                pltpu.VMEM((NY - 1, 16, 128), F32),
                *tp_scratch,
                dma(steps), pltpu.SemaphoreType.DMA, dma(NTP), dma(NTP),
                dma(NY - 1), dma(NY - 1), dma(NY - 1), dma(NY - 1), dma(10), dma(10), dma(sends), dma(sends),
            ],
            compiler_params=pltpu.CompilerParams(collective_id=0, has_side_effects=True, vmem_limit_bytes=big),
            name="token",
        )(table, part, trunk_own, lab_col, lab_row, ids_tile)

        tile = win // 3 if win % 48 == 0 else win
        head = pl.pallas_call(
            functools.partial(head_kernel, nz, stride, tok_total),
            out_shape=jax.ShapeDtypeStruct((nz, win, cols), F32),
            grid=(win // tile,),
            in_specs=[anywhere(), anywhere(), anywhere(), vmem()],
            out_specs=pl.BlockSpec((nz, tile, cols), lambda i: (0, i, 0)),
            scratch_shapes=[
                pltpu.VMEM((win, width), BF16),
                pltpu.VMEM((NY * toks, width), BF16),
                pltpu.VMEM((2, toks, width), F32),
                pltpu.VMEM((tile, NY * toks), BF16),
                pltpu.SemaphoreType.DMA, dma(2),
            ],
            compiler_params=pltpu.CompilerParams(vmem_limit_bytes=big),
            cost_estimate=pl.CostEstimate(flops=4 * NY * toks * win * width, bytes_accessed=40_000_000, transcendentals=0),
            name="head",
        )(table, ub.reshape(toks, width), ub_far.reshape(NY - 1, toks, width), stats)

        row_plan = gather_plan((NX, 1), two_colours(0, own, 1), 16)
        dh_plan = gather_plan((NX, NY), two_colours(0, block, 0.5), block // 4)
        half = 8 * pl.cdiv(win, 16)
        chunks = ((0, half), (half, win))
        share = 0.62 if nz == 8 else 0.5
        table_parts = two_colours(0, half, share) + two_colours(half, win, share, half)
        table_plan = gather_plan((nz, NY), table_parts, 60, {(0, way): half for way in WAYS})
        counts = [2 * len(p[0]) + 1 for p in (row_plan, dh_plan, table_plan)]
        zs = (2, nz // 2 + 1, len(chunks))
        d_rows, loss, stack = pl.pallas_call(
            functools.partial(finish_kernel, nz, stride, vocab_loc, row_plan, dh_plan, table_plan, chunks),
            out_shape=(
                jax.ShapeDtypeStruct((toks, width), BF16),
                jax.ShapeDtypeStruct((8, 128), F32),
                jax.ShapeDtypeStruct((nz, NY, win, cols), F32),
            ),
            in_specs=[vmem(), vmem(), vmem(), vmem(), anywhere()],
            out_specs=(vmem(), vmem(), anywhere()),
            scratch_shapes=[
                *tp_scratch,
                pltpu.VMEM((NTP, NY, block, cols), F32),
                pltpu.VMEM((nz, NY, 16, 128), F32),
                pltpu.VMEM((nz, win, cols), F32),
                pltpu.VMEM((2, nz // 2, win, cols), F32),
                pltpu.VMEM((win, cols), F32),
                dma(10), dma(10), dma(counts[0]), dma(counts[0]), dma(nz), dma(nz), dma(nz), dma(nz),
                dma(counts[1]), dma(counts[1]), dma(*zs), dma(*zs), dma(counts[2]), dma(counts[2]),
                pltpu.SemaphoreType.DMA,
            ],
            compiler_params=pltpu.CompilerParams(collective_id=1, has_side_effects=True, vmem_limit_bytes=67_000_000),
            name="finish",
        )(du, u_own, r_own, tiles, head)
        depth = 8
        chunk = next(n for n in range(224, 0, -8) if stride % n == 0 and NY * stride >= n * depth)
        d_table = pl.pallas_call(
            functools.partial(place_kernel, chunk),
            out_shape=jax.ShapeDtypeStruct((vocab_loc, width), F32),
            in_specs=[anywhere()],
            out_specs=anywhere(),
            scratch_shapes=[pltpu.VMEM((depth, nz, chunk, cols), F32), dma(depth), dma(depth, nz)],
            compiler_params=pltpu.CompilerParams(vmem_limit_bytes=big),
            name="place",
        )(stack)
        mean_loss = loss[0, 0] / tok_total
        return mean_loss, d_rows.reshape(trunk.shape), d_table

    return jax.shard_map(
        per_device,
        mesh=mesh,
        in_specs=(P("tp", None), P("dp", None), P("dp", None), P("dp", None, None)),
        out_specs=(P(), P("dp", None, None), P("tp", None)),
        check_vma=False,
    )
```

time: 1190 us -> 645 us (0.54)
  waiting for transfers between devices: 888 us -> 0 us
  Pallas kernels: 0 us -> 613 us
  blocking collectives: 91.3 us -> 0 us
  matrix products: 70.9 us -> 0 us
  other arithmetic: 66.6 us -> 5.77 us
  local copies, waits for them, and re-layouts: 54.4 us -> 23.3 us
  between operations: 15.6 us -> 2.48 us
    psum x3 -> x0, waiting for transfers between devices: 888 us -> none  [the longest x1 761 us: per_device(): table_grad = lax.psum(table_grad, 'dp')]
    pallas_call x0 -> x4, Pallas kernels: none -> 613 us  [the longest x1 428 us: per_device(): pl.pallas_call(functools.partial(finish_kernel, nz, stride, vocab_loc, ro...]
    psum x2 -> x0, blocking collectives: 77 us -> none  [the longest x1 62.8 us: per_device(): mean_loss = lax.psum(jnp.sum(tok_loss), 'dp') / tok_total]
    dot_general x3 -> x0, matrix products: 70.9 us -> none  [the longest x1 26.3 us: per_device(): lax.dot_general(grad_logits, normed_bf, (((0,), (0,)), ((), ())), preferr...]
    scatter-add x1 -> x0, other arithmetic: 41.7 us -> none  [per_device(): table_grad = head_grad.at[own_ids].add(grad_hidden, mode='drop')]
    unnamed x13 -> x1, local copies, waits for them, and re-layouts: 37.5 us -> 3.16 us
    reduce_sum x5 -> x0, other arithmetic: 15.8 us -> none  [the longest x1 6.81 us: per_device(): sum_exp = lax.psum(jnp.sum(shifted, axis=-1, keepdims=True), 'tp')]
    pmax x1 -> x0, blocking collectives: 14.3 us -> none  [per_device(): row_max = lax.pmax(jnp.max(logits, axis=-1, keepdims=True), 'tp')]
  transfers between devices with their start and end apart: 3 -> 0, of which waited for: 3 -> 0; matrix products, arithmetic and copies ran while one was open for 2% -> 0% of each run, Pallas kernels for 0% -> 0%
where the time goes in v1:
time: 645 us
  Pallas kernels  613 us (95%)
  local copies, waits for them, and re-layouts  23.3 us (4%)
    pallas_call x1, Pallas kernels, per_device(): pl.pallas_call(functools.partial(finish_kernel, nz, stride, vocab_loc, ro...  428 us
    pallas_call x1, Pallas kernels, per_device(): pl.pallas_call(functools.partial(token_kernel, nz, tok_total, token_plan)...  103 us
    pallas_call x1, Pallas kernels, per_device(): pl.pallas_call(functools.partial(head_kernel, nz, stride, tok_total), out...  46.3 us
    pallas_call x1, Pallas kernels, per_device(): pl.pallas_call(functools.partial(place_kernel, chunk), out_shape=jax.Shap...  36.1 us
    gather x1, local copies, waits for them, and re-layouts, per_device(): jnp.take(table, own_ids, axis=0, mode='fill', fill_value=0).astype(F32)  16.2 us

profile of v1, /device:TPU:1, one launch (start us, length us, event | category | flops | bytes accessed | tf_op | source)
XLA Modules:
  0.0 644.9 jit_solution(9326378143185754467)
XLA Ops:
  0.6 0.7 fusion
  1.3 0.1 select_n.64
  1.4 0.1 select_n.66
  1.5 0.7 pad_maximum_fusion.ids
  2.2 1.3 fusion.2
  3.5 0.7 compare_select_fusion
  4.2 1.7 dynamic-slice_bitcast_fusion.trunk
  5.9 0.8 copy.7.lab_col
  6.8 16.2 %gather_fusion = bf16[512,2048]{1,0:T(8,128)(2,1)S(1)} fusion(bf16[6288,2048]{1,0:T(8,128)(2,1)} %table.3, s32[1024]{0:T(1024)S(1)} %pad_clamp_fusion), kind=kCustom, calls=%fused_computation | custom fusion | bytes 4196352 | tf_op jit(solution)/shard_map/jit(_take)/gather | solution.py:742
  23.0 2.4 select_convert_fusion.part
  25.4 102.5 %token_.1 = (f32[512,2048]{1,0:T(8,128)}, f32[8,64,2048]{2,1,0:T(8,128)}, f32[3,8,64,2048]{3,2,1,0:T(8,128)}, f32[64,2048]{1,0:T(8,128)}, f32[64,128]{1,0:T(8,12...) custom-call(bf16[6288,2048]{1,0:T(8,128)(2,1)} %table.3, f32[512,2048]{1,0:T(8,128)} %select_convert_fusion.part, ...), custom_call_target="tpu_custom_call" | custom-call | tf_op jit(solution)/shard_map/token/pallas_call | solution.py:761
  127.9 46.3 %head.1 = f32[8,1584,256]{2,1,0:T(8,128)} custom-call(bf16[6288,2048]{1,0:T(8,128)(2,1)} %table.3, f32[512,2048]{1,0:T(8,128)} %bitcast.16, f32[3,512,2048]{2,1,0:T(8,128)} %bitcast.15, f32[4,8,512]{2,1,0:T(8,128)} %get-tuple-element.19.stats), custom_call_target="tpu_custom_call" | custom-call | flops 26575110144 | bytes 40000000 | tf_op jit(solution)/shard_map/head/pallas_call | solution.py:794
  174.3 428.4 %finish.1 = (bf16[512,2048]{1,0:T(8,128)(2,1)}, f32[8,128]{1,0:T(8,128)}, f32[8,4,1584,256]{3,2,1,0:T(8,128)}) custom-call(f32[512,2048]{1,0:T(8,128)} %get-tuple-element.13.du, f32[64,2048]{1,0:T(8,128)} %get-tuple-element.14.u, f32[64,128]{1,0:T(8,128)} %get-tuple-element.15.r, f32[4,16,128]{2,1,0:T(8,128)} %get-tuple-element.16.tiles, f32[8,1584,256]{2,1,0:T(8,128)} %head.1), custom_call_target="tpu_custom_call" | custom-call | tf_op jit(solution)/shard_map/finish/pallas_call | solution.py:821
  602.6 1.2 slice.3
  604.5 36.1 %place.1 = f32[6288,2048]{1,0:T(8,128)} custom-call(f32[8,4,1584,256]{3,2,1,0:T(8,128)} %get-tuple-element.22.stack), custom_call_target="tpu_custom_call" | custom-call | tf_op jit(solution)/shard_map/place/pallas_call | solution.py:846
  640.6 3.2 copy.9
  (2 shorter events, 0.0 us)

commit v2 on v1

v2 whole, which is shorter than its diff:
```python
import functools
import heapq

import jax
import jax.numpy as jnp
from jax import lax
from jax.experimental import pallas as pl
from jax.experimental.pallas import tpu as pltpu
from jax.sharding import PartitionSpec as P

LN_EPS = 1e-5
MESH = pl.DeviceIdType.MESH
F32, BF16 = jnp.float32, jnp.bfloat16
NY, NTP, NX = 4, 8, 4
WAYS = (1, -1)
PACE = ((10, 0), (20, 15), (20, 26))
SHARES = (0.55, 0.55, 0.7)
ALL = Ellipsis
NEG = float(jnp.finfo(jnp.float32).min)
VT = 512
NT_DIMS = (((1,), (1,)), ((), ()))
NN_DIMS = (((1,), (0,)), ((), ()))


def rem(a, b):
    return lax.rem(a, jnp.int32(b))


class Place:
    def __init__(self, nz):
        self.nz = nz
        self.dp = lax.axis_index("dp")
        self.tp = lax.axis_index("tp")
        self.z, self.y = lax.div(self.dp, jnp.int32(NY)), rem(self.dp, NY)
        self.x, self.c = lax.div(self.tp, jnp.int32(2)), rem(self.tp, 2)
        self.partner = 2 * self.x + (1 - self.c)

    def tp_of(self, step, other=False):
        c = 1 - self.c if other else self.c
        return 2 * rem(self.x + step + NX, NX) + c

    def y_of(self, step):
        return rem(self.y + step + NY, NY)

    def dp_of_y(self, step):
        return self.z * NY + self.y_of(step)

    def dp_of_z(self, step):
        return rem(self.z + step + self.nz, self.nz) * NY + self.y


def to_tp(tp):
    return {"tp": tp}


def to_dp(dp):
    return {"dp": dp}


def rdma(src, dst, send_sem, recv_sem, device):
    return pltpu.make_async_remote_copy(
        src_ref=src, dst_ref=dst, send_sem=send_sem, recv_sem=recv_sem, device_id=device, device_id_type=MESH
    )


def greet(devices):
    barrier = pltpu.get_barrier_semaphore()
    for device in devices:
        pl.semaphore_signal(barrier, inc=1, device_id=device, device_id_type=MESH)
    pl.semaphore_wait(barrier, len(devices))


class SumTp:
    def __init__(self, at, src, own, pb, rl, fin, send, recv):
        self.src, self.own, self.half, self.pb, self.rl, self.fin = src, own, own // 2, pb, rl, fin
        self.at, self.send, self.recv = at, send, recv
        self.steps = (2, 1, -1, 0)
        self.copies = []

    def copy(self, i, src, dst, tp):
        self.copies.append(rdma(src, dst, self.send.at[i], self.recv.at[i], to_tp(tp)))
        return self.copies[-1]

    def rows(self, step, other):
        return pl.ds(pl.multiple_of(self.at.tp_of(step, other) * self.own, self.own), self.own)

    def part(self, i, h):
        return self.pb.at[i, pl.ds(h * self.half, self.half)]

    def begin(self):
        for i, step in enumerate(self.steps):
            self.copy(i, self.src.at[self.rows(step, True)], self.pb.at[i], self.at.partner).start()

    def merge(self, i):
        self.copies[i].wait_recv()
        self.pb[i] = self.pb[i] + self.src[self.rows(self.steps[i], False), :]

    def pass_on(self):
        plus, minus = self.at.tp_of(1), self.at.tp_of(-1)
        self.merge(0)
        for h, tp in enumerate((plus, minus)):
            self.copy(4 + h, self.part(0, h), self.rl.at[h], tp).start()
        self.merge(1)
        self.merge(2)
        self.copy(6, self.part(1, 1), self.fin.at[0], plus).start()
        self.copy(7, self.part(2, 0), self.fin.at[1], minus).start()

    def join(self):
        for h, tp in enumerate((self.at.tp_of(1), self.at.tp_of(-1))):
            self.copies[4 + h].wait_recv()
            rows = pl.ds(h * self.half, self.half)
            self.pb[1 + h, rows] = self.pb[1 + h, rows] + self.rl[h]
            self.copy(8 + h, self.part(1 + h, h), self.fin.at[2 + h], tp).start()
        self.merge(3)

    def result(self):
        for copy in self.copies[6:]:
            copy.wait_recv()
        top = self.pb[3, 0 : self.half] + self.fin[2] + self.fin[1]
        low = self.pb[3, self.half : self.own] + self.fin[0] + self.fin[3]
        for copy in self.copies:
            copy.wait_send()
        return jnp.concatenate([top, low], axis=0)


def gather_plan(sizes, parts, latency, hold=0):
    sends, events, heap, busy = [], [], [], {}

    def post(axis, way, off, lo, hi, order, now):
        end = max(now, busy.get((axis, way), now)) + hi - lo
        busy[axis, way] = end
        there = tuple(o - way * (a == axis) for a, o in enumerate(off))
        heapq.heappush(heap, (end + latency, len(sends), there, lo, hi, order))
        sends.append((axis, way, off, lo, hi))
        return len(sends) - 1

    def ring(axis, way, off, lo, hi, order, now):
        last = sizes[axis] // 2
        gone = abs(off[axis]) + 1
        if gone > last:
            return []
        if gone == last:
            mid = lo + 8 * pl.cdiv(hi - lo, 16)
            lo, hi = (lo, mid) if way > 0 else (mid, hi)
        return [] if lo == hi else [post(axis, way, off, lo, hi, order, now)]

    starts = [[] for _ in parts]
    for leg in range(2):
        for begin, (lo, hi, order, now) in zip(starts, parts):
            for way in WAYS:
                begin += ring(order[leg], way, (0, 0), lo, hi, order, now)
    while heap:
        now, i, off, lo, hi, order = heapq.heappop(heap)
        axis, way = sends[i][:2]
        if off[1] and now < hold:
            heapq.heappush(heap, (hold, i, off, lo, hi, order))
            continue
        new = ring(axis, way, off, lo, hi, order, now)
        if axis == order[0]:
            for w in WAYS:
                new += ring(order[1], w, off, lo, hi, order, now)
        events.append((i, new, now))
    return sends, starts, events


def two_colours(lo, hi, share, now=0):
    split = lo + 8 * round((hi - lo) * share / 8)
    return [(lo, split, (0, 1), now), (split, hi, (1, 0), now)]


class Spread:
    def __init__(self, at, plan, rows, block, send, recv):
        self.sends, self.starts, self.events = plan
        self.block, self.send, self.recv, self.rows = block, send, recv, rows
        self.count = len(self.sends)
        self.other = to_tp(at.partner)
        self.device = {}
        for way in WAYS:
            self.device[0, way] = to_tp(at.tp_of(way))
            self.device[1, way] = to_dp(at.dp_of_y(way))

    def goal(self, i):
        axis, way, off = self.sends[i][:3]
        return tuple(o - way * (a == axis) for a, o in enumerate(off))

    def copy(self, i):
        axis, way, off, lo, hi = self.sends[i]
        src, dst = self.block(*off, False, lo, hi), self.block(off[0], self.goal(i)[1], False, lo, hi)
        return rdma(src, dst, self.send.at[i], self.recv.at[i], self.device[axis, way])

    def forward(self, i, cross=False):
        off, (lo, hi) = ((0, 0), (0, self.rows)) if i == self.count else (self.goal(i), self.sends[i][-2:])
        ref = self.block(*off, cross, lo, hi)
        return rdma(ref, ref, self.send.at[self.count + i], self.recv.at[self.count + i], self.other)

    def begin(self):
        for i in sum(self.starts, []):
            self.copy(i).start()
        self.forward(self.count).start()

    def run(self, events):
        for i, new, _ in events:
            ref = self.block(*self.goal(i), False, *self.sends[i][-2:])
            rdma(ref, ref, self.send.at[i], self.recv.at[i], self.other).wait_recv()
            for j in new:
                self.copy(j).start()
            self.forward(i).start()

    def take(self, i):
        self.forward(i, True).wait_recv()

    def end(self):
        for i in range(self.count):
            self.copy(i).wait_send()
        for i in range(self.count + 1):
            self.forward(i).wait_send()


def token_kernel(
    nz, tok_total, plan, table, part, trunk, marks, lab_row, ids,
    du, ub_all, u_out, r_out, stats, tiles,
    table_v, ub_v, z_v, run, mine, theirs, row_out, row_in, tile_out, tile_in, pb, rl, fin, land,
    load_sem, part_sem, st_send, st_recv, row_send, row_recv, t_send, t_recv, rs_send, rs_recv, x_send, x_recv,
):
    at = Place(nz)
    rows, width = table_v.shape
    toks = ub_v.shape[0]
    own = trunk.shape[0]
    steps = z_v.shape[0]
    whole = rows // VT
    tail = rows - whole * VT

    part_copy = pltpu.make_async_copy(part, ub_v, part_sem)
    part_copy.start()

    def load(i):
        start = pl.multiple_of(i * VT, 16)
        return pltpu.make_async_copy(table.at[pl.ds(start, VT)], table_v.at[pl.ds(start, VT)], load_sem.at[i])

    tail_copy = pltpu.make_async_copy(
        table.at[pl.ds(whole * VT, tail)], table_v.at[pl.ds(whole * VT, tail)], load_sem.at[whole]
    )
    greet([to_tp(rem(at.tp + i, NTP)) for i in range(1, NTP)] + [to_dp(at.dp_of_y(i)) for i in range(1, NY)])
    part_copy.wait()
    for i in range(whole):
        load(i).start()
    tail_copy.start()
    mine_only = (marks[:, 1:2] >= 0) & (marks[:, 1:2] < rows)
    du[ALL] = jnp.where(mine_only, ub_v[ALL].astype(F32), 0.0)
    sums = SumTp(at, du, own, pb, rl, fin, rs_send, rs_recv)
    sums.begin()
    sums.pass_on()
    sums.join()
    hidden = sums.result() + trunk[ALL].astype(F32)
    centered = hidden - jnp.mean(hidden, axis=-1, keepdims=True)
    inv_std = lax.rsqrt(jnp.mean(centered * centered, axis=-1, keepdims=True) + LN_EPS)
    normed = centered * inv_std
    land[at.tp] = normed.astype(BF16).astype(F32)

    def block(dx, dy, cross, lo, hi):
        tp, cut = at.tp_of(dx, cross), pl.ds(lo, hi - lo)
        return ub_all.at[dy % NY, tp, cut] if dy % NY else land.at[tp, cut]

    spread = Spread(at, plan, own, block, x_send, x_recv)
    spread.begin()
    u_out[ALL] = normed
    r_out[ALL] = jnp.broadcast_to(inv_std, r_out.shape)
    near = [e for e in spread.events if spread.goal(e[0])[1] == 0]
    spread.run(near)
    for e in near:
        spread.take(e[0])
    spread.take(spread.count)
    groups = {}
    pace = own / 7.5
    for e in [e for e in spread.events if e not in near]:
        due = max(0, int((e[-1] - near[-1][-1]) / pace)) + 2
        groups.setdefault(due if due <= steps else max(steps, due - 5), []).append(e)
    late = [e for due in sorted(groups) if due >= 2 * steps for e in groups[due]]

    def attend(step):
        for due, events in groups.items():
            if due < 2 * steps:

                @pl.when(step == due)
                def _(events=events):
                    spread.run(events)

    keep = pltpu.make_async_copy(land, ub_all.at[0], part_sem)
    keep.start()
    ub_v[ALL] = land[ALL].reshape(toks, width).astype(BF16)
    run[0] = jnp.full(run.shape[1:], NEG, F32)
    run[1] = jnp.zeros(run.shape[1:], F32)
    lane = lax.broadcasted_iota(jnp.int32, (toks, VT), 1)

    def start_of(i):
        return pl.multiple_of(jnp.minimum(i * VT, rows - VT), 16)

    def fold(op, v):
        return functools.reduce(op, [v[:, j : j + 128] for j in range(0, VT, 128)])

    def forward(i, carry):
        attend(i)

        @pl.when(i < whole)
        def _():
            load(i).wait()

        @pl.when(i == whole)
        def _():
            tail_copy.wait()

        start = start_of(i)
        z = lax.dot_general(ub_v[ALL], table_v[pl.ds(start, VT), :], NT_DIMS, preferred_element_type=F32)
        z = jnp.where(lane >= i * VT - start, z, NEG)
        z_v[i] = z
        run[0] = jnp.maximum(run[0], fold(jnp.maximum, z))
        hit = (lane + start == marks[:, 0:1]) & (lane >= i * VT - start)
        run[1] = run[1] + fold(jnp.add, jnp.where(hit, z, 0.0))
        return carry

    lax.fori_loop(0, steps, forward, 0)
    top = jnp.max(run[0], axis=1, keepdims=True)
    run[0] = jnp.zeros(run.shape[1:], F32)

    def exps(i, carry):
        run[0] = run[0] + fold(jnp.add, jnp.exp(z_v[i] - top))
        return carry

    lax.fori_loop(0, steps, exps, 0)
    total = jnp.sum(run[0], axis=1, keepdims=True)
    label = jnp.sum(run[1], axis=1, keepdims=True)
    narrow = lax.broadcasted_iota(jnp.int32, (toks, 128), 1)
    packed = jnp.where(narrow == 0, top, jnp.where(narrow == 1, total, jnp.where(narrow == 2, label, 0.0)))
    mine[ALL] = jnp.transpose(packed)[:8]
    stat = []
    for i in range(1, NTP):
        stat.append(rdma(mine, theirs.at[i], st_send.at[i], st_recv.at[i], to_tp(rem(at.tp + i, NTP))))
        stat[-1].start()
    theirs[0] = mine[ALL]
    for copy in stat:
        copy.wait_recv()
    parts = [theirs[rem(at.tp - j + NTP, NTP)] for j in range(NTP)]
    peak = functools.reduce(jnp.maximum, [p[0:1] for p in parts])
    total = functools.reduce(jnp.add, [p[1:2] * jnp.exp(p[0:1] - peak) for p in parts])
    label = functools.reduce(jnp.add, [p[2:3] for p in parts])
    lse = peak + jnp.log(total)
    loss = jnp.sum(jnp.log(total) + peak - label, axis=1, keepdims=True)
    sub = lax.broadcasted_iota(jnp.int32, (8, toks), 0)
    row_out[ALL] = jnp.where(sub == 0, lse, jnp.where(sub == 1, lab_row[ALL], 0.0))
    upper = lax.broadcasted_iota(jnp.int32, ids.shape, 1) >= 64
    tile_out[ALL] = jnp.where(upper == (rem(at.z, 2) == 1), ids[ALL], loss)
    tiles[0] = tile_out[ALL]
    rows_sent = []
    for i in range(NY - 1):
        to_y = to_dp(at.dp_of_y(NY - 1 - i))
        rows_sent.append(rdma(row_out, row_in.at[i], row_send.at[i], row_recv.at[i], to_y))
        rows_sent.append(rdma(tile_out, tile_in.at[i], t_send.at[i], t_recv.at[i], to_y))
    for copy in rows_sent:
        copy.start()
    run[0] = jnp.transpose(jnp.broadcast_to(lse, (128, toks)))
    wide = min(512, width)
    inv_total = 1.0 / tok_total
    du[ALL] = jnp.zeros(du.shape, F32)

    def backward(i, carry):
        attend(i + steps)
        start = start_of(i)
        shift = jnp.concatenate([run[0]] * (VT // 128), axis=1)
        prob = jnp.exp(z_v[i] - shift)
        hit = (lane + start == marks[:, 0:1]) & (lane >= i * VT - start)
        grad = ((prob - jnp.where(hit, 1.0, 0.0)) * inv_total).astype(BF16)
        for n in range(width // wide):
            cols = pl.ds(n * wide, wide)
            du[:, cols] = du[:, cols] + lax.dot_general(
                grad, table_v[pl.ds(start, VT), cols], NN_DIMS, preferred_element_type=F32
            )
        return carry

    lax.fori_loop(0, steps, backward, 0)
    spread.run(late)
    for e in spread.events:
        if e not in near:
            spread.take(e[0])
    for copy in rows_sent:
        copy.wait_recv()
    stats[0] = row_out[ALL]
    for i in range(NY - 1):
        stats[i + 1] = row_in[i]
        tiles[i + 1] = tile_in[i]
    keep.wait()
    spread.end()
    for copy in stat + rows_sent:
        copy.wait_send()


class SumZ:
    def __init__(self, at, parts, came, total, chunks, send, recv):
        self.at, self.parts, self.came, self.total = at, parts, came, total
        self.chunks, self.send, self.recv = chunks, send, recv
        self.last = at.nz // 2

    def rows(self, c, s, way):
        lo, hi = self.chunks[c]
        if s == 1:
            mid = lo + 8 * pl.cdiv(hi - lo, 16)
            lo, hi = (lo, mid) if way > 0 else (mid, hi)
        return pl.ds(lo, hi - lo)

    def slot(self, s, way):
        return 0 if s == 1 else 2 * (s - 1) - (way > 0)

    def goal(self, s, way):
        return rem(self.at.z + way * (self.last + 1 - s) + self.at.nz, self.at.nz)

    def copy(self, c, s, way):
        rows, w = self.rows(c, s, way), WAYS.index(way)
        sems = self.send.at[w, s, c], self.recv.at[w, s, c]
        src = self.parts.at[self.goal(s, way), rows]
        return rdma(src, self.came.at[self.slot(s, way), rows], *sems, to_dp(self.at.dp_of_z(way)))

    def begin(self, c):
        rows = pl.ds(self.chunks[c][0], self.chunks[c][1] - self.chunks[c][0])
        self.total[rows] = self.parts[self.at.z, rows]
        for way in WAYS:
            self.copy(c, 1, way).start()

    def run(self, c, s):
        for way in WAYS:
            self.copy(c, s, way).wait_recv()
            rows, slot = self.rows(c, s, way), self.slot(s, way)
            if s < self.last:
                goal = self.goal(s + 1, way)
                self.parts[goal, rows] = self.parts[goal, rows] + self.came[slot, rows]
                self.copy(c, s + 1, way).start()
            else:
                self.total[rows] = self.total[rows] + self.came[slot, rows]

    def end(self):
        for c in range(len(self.chunks)):
            for s in range(self.last):
                for way in WAYS:
                    self.copy(c, s + 1, way).wait_send()


def finish_kernel(
    nz, stride, vocab_loc, tok_total, row_plan, dh_plan, table_plan, chunks,
    table, ub, stats, du, u, r, tiles,
    d_trunk, loss, stack, all_dh,
    pb, rl, fin, land, all_tiles, table_v, ub_v, stage, grad_v, parts, came, total, dh_v,
    rs_send, rs_recv, row_send, row_recv, z_send, z_recv, i_send, i_recv, x_send, x_recv, s_send, s_recv, t_send, t_recv,
    load_sem, stage_sem, dh_sem,
):
    at = Place(nz)
    own, width = u.shape
    win, cols = total.shape
    toks = stats.shape[2]
    block = nz * own
    slab = stage.shape[1]
    first = pl.multiple_of(at.y * stride, 16)
    load = pltpu.make_async_copy(table.at[pl.ds(first, win)], table_v, load_sem)

    depth, per = stage.shape[0], toks // slab
    slabs = NY * per

    def fill(i):
        rows = pl.ds(pl.multiple_of(rem(i, per) * slab, slab), slab)
        at_slot = rem(i, depth)
        return pltpu.make_async_copy(ub.at[lax.div(i, jnp.int32(per)), rows], stage.at[at_slot], stage_sem.at[at_slot])

    for i in range(depth):
        fill(jnp.int32(i)).start()
    load.start()
    greet(
        [to_tp(rem(at.tp + i, NTP)) for i in range(1, NTP)]
        + [to_dp(at.dp_of_z(i)) for i in range(1, nz)]
        + [to_dp(at.dp_of_y(way)) for way in WAYS]
    )
    sum_tp = SumTp(at, du, own, pb, rl, fin, rs_send, rs_recv)
    sum_tp.begin()

    def narrow(n):
        def body(k, carry):
            i = n * per + k
            fill(i).wait()
            ub_v[pl.ds(pl.multiple_of(i * slab, slab), slab)] = stage[rem(i, depth)].astype(BF16)

            @pl.when(i + depth < slabs)
            def _():
                fill(i + depth).start()

            return carry

        lax.fori_loop(0, per, body, 0)

    narrow(0)
    sum_tp.pass_on()
    load.wait()

    inv_total = 1.0 / tok_total

    def logits(lo, hi, ahead=lambda n: None):
        vocab = at.tp * vocab_loc + first + lo + lax.broadcasted_iota(jnp.int32, (hi - lo, toks), 0)

        def body(n, carry):
            ahead(n)
            cut = pl.ds(pl.multiple_of(n * toks, 128), toks)
            z = lax.dot_general(table_v[lo:hi, :], ub_v[cut, :], NT_DIMS, preferred_element_type=F32)
            row = stats[n]
            prob = jnp.exp(z - row[0:1])
            hit = vocab == row[1:2].astype(jnp.int32)
            grad_v[0 : hi - lo, cut] = ((prob - jnp.where(hit, 1.0, 0.0)) * inv_total).astype(BF16)
            return carry

        lax.fori_loop(0, NY, body, 0)

    def head(lo, hi):
        def body(n, carry):
            cut = pl.ds(pl.multiple_of(n * cols, 128), cols)
            parts[n, lo:hi] = jnp.dot(grad_v[0 : hi - lo, :], ub_v[:, cut], preferred_element_type=F32)
            return carry

        lax.fori_loop(0, nz, body, 0)

    sums = SumZ(at, parts, came, total, chunks, s_send, s_recv)
    todo = [(c, s) for _, c, s in sorted((k * s + late, c, s) for s in range(1, sums.last + 1) for c, (k, late) in enumerate(PACE))]

    def narrow_next(n):
        @pl.when(n + 1 < NY)
        def _():
            narrow(n + 1)

    logits(*chunks[0], narrow_next)
    head(*chunks[0])
    sums.begin(0)
    sum_tp.join()
    logits(*chunks[1])
    sums.run(*todo[0])
    grad = sum_tp.result()
    normed = u[ALL]
    mean_g = jnp.mean(grad, axis=-1, keepdims=True)
    mean_gu = jnp.mean(grad * normed, axis=-1, keepdims=True)
    land[at.tp] = r[:, 0:1] * (grad - mean_g - normed * mean_gu)

    def row_block(dx, dy, cross, lo, hi):
        return land.at[at.tp_of(dx, cross), pl.ds(lo, hi - lo)]

    whole_rows = Spread(at, row_plan, own, row_block, row_send, row_recv)
    whole_rows.begin()
    here = pl.ds(pl.multiple_of(at.z * own, own), own)
    turned = []
    for i in range(1, nz):
        col, to_z = pl.multiple_of(rem(at.z + i, nz) * cols, 128), to_dp(at.dp_of_z(i))
        src = land.at[at.tp, :, pl.ds(col, cols)]
        turned.append(rdma(src, all_dh.at[at.tp, 0, here], z_send.at[i], z_recv.at[i], to_z))
        turned.append(rdma(tiles, all_tiles.at[at.z], i_send.at[i], i_recv.at[i], to_z))
    for copy in turned:
        copy.start()
    my_col = pl.multiple_of(at.z * cols, 128)
    mine = pltpu.make_async_copy(land.at[at.tp, :, pl.ds(my_col, cols)], all_dh.at[at.tp, 0, here], load_sem)
    mine.start()
    all_tiles[at.z] = tiles[ALL]
    head(*chunks[1])
    sums.begin(1)
    sums.run(*todo[1])
    logits(*chunks[2])
    whole_rows.run(whole_rows.events)
    mine.wait()
    for copy in turned:
        copy.wait_recv()

    def dh_block(dx, dy, cross, lo, hi):
        return all_dh.at[at.tp_of(dx, cross), dy % NY, pl.ds(lo, hi - lo)]

    blocks = Spread(at, dh_plan, block, dh_block, x_send, x_recv)
    blocks.begin()
    head(*chunks[2])
    sums.begin(2)

    pieces = {(0, 0): [(blocks.count, [], 0)]}
    for e in blocks.events:
        dx, dy = blocks.goal(e[0])
        pieces.setdefault((dx % NX, dy % NY), []).append(e)
    order = sorted((pieces[p][-1][-1] + cross * (block // 3), *p, cross) for p in pieces for cross in range(2))
    left = list(blocks.events)
    due = []
    for time, dx, dy, cross in order:
        due.append([e for e in left if e[-1] <= time])
        left = [e for e in left if e[-1] > time]
    code = [dx + NX * (dy + NY * cross) for _, dx, dy, cross in order]
    ready = 2

    def meet(k):
        blocks.run(due[k])
        _, dx, dy, cross = order[k]
        if cross:
            for part in pieces[dx, dy]:
                blocks.take(part[0])

    for k in range(ready):
        meet(k)
    for i in range(whole_rows.count + 1):
        whole_rows.take(i)
    d_trunk[ALL] = land[ALL].reshape(d_trunk.shape).astype(BF16)
    upper = lax.broadcasted_iota(jnp.int32, loss.shape, 1) >= 64
    loss[ALL] = sum(
        jnp.where(upper == (z % 2 == 0), all_tiles[z, rem(y - at.y + NY, NY)], 0.0) for z in range(nz) for y in range(NY)
    )

    beside = {at_piece: todo[2 + k] for k, at_piece in enumerate((0, 1, 4, 7, 15, 24)) if 2 + k < len(todo)}
    low = (at.tp * vocab_loc + at.y * stride).astype(F32)

    def place_of(e):
        mark = jnp.int32(code[0])
        for k in range(1, len(order)):
            mark = jnp.where(e == k, code[k], mark)
        core = jnp.where(mark >= NX * NY, 1 - at.c, at.c)
        return 2 * rem(at.x + rem(mark, NX), NX) + core, rem(lax.div(mark, jnp.int32(NX)), NY)

    def fetch(e):
        tp, far = place_of(e)
        half = rem(e, 2)
        return pltpu.make_async_copy(all_dh.at[tp, far], dh_v.at[half], dh_sem.at[half])

    def piece(e, carry):
        for k in range(len(order)):
            met = k + 1 if k + 1 < len(order) and k + 1 >= ready else 0
            if k in beside or met:

                @pl.when(e == k)
                def _(k=k, met=met):
                    if k in beside:
                        sums.run(*beside[k])
                    if met:
                        meet(met)

        @pl.when(e + 1 < len(order))
        def _():
            fetch(e + 1).start()

        tp, far = place_of(e)
        ids = jnp.concatenate(
            [
                jnp.where(upper[0:1], all_tiles[2 * j + 1, far, pl.ds(tp, 1), :], all_tiles[2 * j, far, pl.ds(tp, 1), :])
                for j in range(nz // 2)
            ],
            axis=1,
        )
        fetch(e).wait()
        dh = dh_v[rem(e, 2)]
        hi = dh.astype(BF16)
        rest = dh - hi.astype(F32)
        mid = rest.astype(BF16)
        lo = (rest - mid.astype(F32)).astype(BF16)
        ids = (ids - low).astype(jnp.int32)
        for begin, end in chunks:
            row = lax.broadcasted_iota(jnp.int32, (end - begin, block), 0) + begin
            pick = jnp.where(row == ids, 1.0, 0.0).astype(BF16)
            found = sum(jnp.dot(pick, term, preferred_element_type=F32) for term in (hi, mid, lo))
            total[begin:end] = total[begin:end] + found
        return carry

    fetch(jnp.int32(0)).start()
    lax.fori_loop(0, len(order), piece, 0)
    for copy in turned:
        copy.wait_send()

    sends, starts, events = table_plan
    device = {(0, way): to_dp(at.dp_of_z(way)) for way in WAYS} | {(1, way): to_dp(at.dp_of_y(way)) for way in WAYS}

    def copy_of(i, arrives=False):
        axis, way, off, lo, hi = sends[i]
        if arrives:
            off = tuple(o - way * (a == axis) for a, o in enumerate(off))
        dst = stack.at[rem(at.z + off[0] + nz, nz), at.y_of(off[1]), pl.ds(lo, hi - lo)]
        src = dst if any(off) else total.at[pl.ds(lo, hi - lo)]
        return rdma(src, dst, t_send.at[i], t_recv.at[i], device[axis, way])

    for step in todo[2 + len(beside) :]:
        sums.run(*step)
    for i in sum(starts, []):
        copy_of(i).start()
    keep = pltpu.make_async_copy(total, stack.at[at.z, at.y], load_sem)
    keep.start()
    for i, new, _ in events:
        copy_of(i, True).wait_recv()
        for j in new:
            copy_of(j).start()
    keep.wait()
    for i in range(len(sends)):
        copy_of(i).wait_send()
    sums.end()
    whole_rows.end()
    blocks.end()


def place_kernel(chunk, tok_total, stack, rows_in, loss_in, out, rows_out, loss_out, slots, rows_v, load_sem, store_sem, rows_sem):
    nz, ny, have, cols = stack.shape
    depth = slots.shape[0]
    per = have // chunk
    total = ny * per
    ahead = depth // 2

    def load(i):
        y, row = lax.div(i, jnp.int32(per)), pl.multiple_of(rem(i, per) * chunk, 8)
        s = rem(i, depth)
        return pltpu.make_async_copy(stack.at[:, y, pl.ds(row, chunk)], slots.at[s], load_sem.at[s])

    def stores(i):
        s, row = rem(i, depth), pl.multiple_of(i * chunk, 8)
        return [
            pltpu.make_async_copy(slots.at[s, j], out.at[pl.ds(row, chunk), pl.ds(j * cols, cols)], store_sem.at[s, j])
            for j in range(nz)
        ]

    def prime(i, carry):
        load(i).start()
        return carry

    def body(i, carry):
        load(i).wait()
        for copy in stores(i):
            copy.start()

        @pl.when(i + ahead < total)
        def _():
            @pl.when(i >= ahead)
            def _():
                for copy in stores(i - ahead):
                    copy.wait()

            load(i + ahead).start()

        return carry

    def drain(i, carry):
        for copy in stores(i):
            copy.wait()
        return carry

    rows_load = pltpu.make_async_copy(rows_in, rows_v, rows_sem)
    rows_store = pltpu.make_async_copy(rows_v, rows_out, rows_sem)
    lax.fori_loop(0, ahead, prime, 0)
    rows_load.start()
    lane = lax.broadcasted_iota(jnp.int32, (1, 128), 1)
    loss_out[0, 0] = jnp.sum(jnp.where(rem(lane, 64) == 0, loss_in[0:1], 0.0)) / tok_total
    rows_load.wait()
    rows_store.start()
    lax.fori_loop(0, total, body, 0)
    lax.fori_loop(total - 2 * ahead, total, drain, 0)
    used = per * chunk
    left = have - used
    rest = pltpu.make_async_copy(stack.at[:, ny - 1, pl.ds(used, left)], slots.at[0, :, pl.ds(0, left)], load_sem.at[0])
    rest.start()
    rest.wait()
    tails = [
        pltpu.make_async_copy(
            slots.at[0, j, pl.ds(0, left)], out.at[pl.ds(ny * used, left), pl.ds(j * cols, cols)], store_sem.at[0, j]
        )
        for j in range(nz)
    ]
    for copy in tails:
        copy.start()
    for copy in tails:
        copy.wait()
    rows_store.wait()


def vmem():
    return pl.BlockSpec(memory_space=pltpu.VMEM)


def anywhere():
    return pl.BlockSpec(memory_space=pl.ANY)


def dma(*shape):
    return pltpu.SemaphoreType.DMA(shape)


def solution(mesh):
    ndp, ntp = mesh.shape["dp"], mesh.shape["tp"]
    nz = ndp // NY

    def per_device(table, ids, labels, trunk):
        vocab_loc, width = table.shape
        batch, seq = ids.shape
        toks = batch * seq
        own = toks // NTP
        tok_total = toks * ndp
        stride = (vocab_loc - 16) // NY
        win = stride + 16
        cols = width // nz
        block = nz * own
        big = 66_000_000
        dp, tp = lax.axis_index("dp"), lax.axis_index("tp")
        row_start = tp * vocab_loc
        local_ids = ids.reshape(toks) - row_start
        part = jnp.take(table, local_ids, axis=0, mode="clip")
        trunk_own = lax.dynamic_slice_in_dim(trunk.reshape(toks, width), tp * own, own, 0)

        tp_scratch = [
            pltpu.VMEM((4, own, width), F32),
            pltpu.VMEM((2, own // 2, width), F32),
            pltpu.VMEM((4, own // 2, width), F32),
            pltpu.VMEM((NTP, own, width), F32),
        ]
        ids_f = ids.reshape(NTP, own).astype(F32)
        blank = jnp.zeros_like(ids_f)
        even = rem(lax.div(dp, jnp.int32(NY)), 2) == 0
        pad = ((0, 0), (0, 128 - 2 * own))
        ids_tile = jnp.pad(jnp.concatenate([jnp.where(even, ids_f, blank), jnp.where(even, blank, ids_f)], axis=1), pad)
        marks = jnp.stack([labels.reshape(toks) - row_start, local_ids], axis=1)
        lab_row = labels.reshape(1, toks).astype(F32)
        steps = pl.cdiv(vocab_loc, VT)
        token_plan = gather_plan((NX, NY), two_colours(0, own, 0.5), 16, hold=2 * own)
        sends = 2 * len(token_plan[0]) + 1
        du, ub, u_own, r_own, stats, tiles = pl.pallas_call(
            functools.partial(token_kernel, nz, tok_total, token_plan),
            out_shape=(
                jax.ShapeDtypeStruct((toks, width), F32),
                jax.ShapeDtypeStruct((NY, NTP, own, width), F32),
                jax.ShapeDtypeStruct((own, width), F32),
                jax.ShapeDtypeStruct((own, 128), F32),
                jax.ShapeDtypeStruct((NY, 8, toks), F32),
                jax.ShapeDtypeStruct((NY, 8, 128), F32),
            ),
            in_specs=[anywhere(), anywhere(), vmem(), vmem(), vmem(), vmem()],
            out_specs=(vmem(), anywhere(), vmem(), vmem(), vmem(), vmem()),
            scratch_shapes=[
                pltpu.VMEM((vocab_loc, width), BF16),
                pltpu.VMEM((toks, width), BF16),
                pltpu.VMEM((steps, toks, VT), F32),
                pltpu.VMEM((2, toks, 128), F32),
                pltpu.VMEM((8, toks), F32),
                pltpu.VMEM((NTP, 8, toks), F32),
                pltpu.VMEM((8, toks), F32),
                pltpu.VMEM((NY - 1, 8, toks), F32),
                pltpu.VMEM((8, 128), F32),
                pltpu.VMEM((NY - 1, 8, 128), F32),
                *tp_scratch,
                dma(steps), pltpu.SemaphoreType.DMA, dma(NTP), dma(NTP),
                dma(NY - 1), dma(NY - 1), dma(NY - 1), dma(NY - 1), dma(10), dma(10), dma(sends), dma(sends),
            ],
            compiler_params=pltpu.CompilerParams(collective_id=0, has_side_effects=True, vmem_limit_bytes=big),
            name="token",
        )(table, part, trunk_own, marks, lab_row, ids_tile)

        row_plan = gather_plan((NX, 1), two_colours(0, own, 1), 16)
        dh_plan = gather_plan((NX, NY), two_colours(0, block, 0.5), block // 4)
        lead = 16 * (win // 96)
        middle = lead + 16 * pl.cdiv(win - lead, 32)
        chunks = ((0, lead), (lead, middle), (middle, win))
        third = 8 * pl.cdiv(win, 24)
        table_chunks = ((0, third), (third, 2 * third), (2 * third, win))
        shares = SHARES if nz == 8 else (0.5,) * 3
        table_parts = sum((two_colours(lo, hi, share) for (lo, hi), share in zip(table_chunks, shares)), [])
        table_plan = gather_plan((nz, NY), table_parts, 60)
        counts = [2 * len(p[0]) + 1 for p in (row_plan, dh_plan, table_plan)]
        zs = (2, nz // 2 + 1, len(chunks))
        d_rows, loss, stack, _ = pl.pallas_call(
            functools.partial(
                finish_kernel, nz, stride, vocab_loc, tok_total, row_plan, dh_plan, table_plan, chunks
            ),
            out_shape=(
                jax.ShapeDtypeStruct((toks, width), BF16),
                jax.ShapeDtypeStruct((8, 128), F32),
                jax.ShapeDtypeStruct((nz, NY, win, cols), F32),
                jax.ShapeDtypeStruct((NTP, NY, block, cols), F32),
            ),
            in_specs=[anywhere(), anywhere(), vmem(), vmem(), vmem(), vmem(), vmem()],
            out_specs=(vmem(), vmem(), anywhere(), anywhere()),
            scratch_shapes=[
                *tp_scratch,
                pltpu.VMEM((nz, NY, 8, 128), F32),
                pltpu.VMEM((win, width), BF16),
                pltpu.VMEM((NY * toks, width), BF16),
                pltpu.VMEM((4, 128, width), F32),
                pltpu.VMEM((middle - lead, NY * toks), BF16),
                pltpu.VMEM((nz, win, cols), F32),
                pltpu.VMEM((nz - 1, win, cols), F32),
                pltpu.VMEM((win, cols), F32),
                pltpu.VMEM((2, block, cols), F32),
                dma(10), dma(10), dma(counts[0]), dma(counts[0]), dma(nz), dma(nz), dma(nz), dma(nz),
                dma(counts[1]), dma(counts[1]), dma(*zs), dma(*zs), dma(counts[2]), dma(counts[2]),
                pltpu.SemaphoreType.DMA, dma(4), dma(2),
            ],
            compiler_params=pltpu.CompilerParams(collective_id=1, has_side_effects=True, vmem_limit_bytes=67_000_000),
            name="finish",
        )(table, ub.reshape(NY, toks, width), stats, du, u_own, r_own, tiles)
        depth = 8
        chunk = next(n for n in range(224, 0, -8) if stride % n == 0 and NY * stride >= n * depth)
        d_table, d_rows, mean_loss = pl.pallas_call(
            functools.partial(place_kernel, chunk, tok_total),
            out_shape=(
                jax.ShapeDtypeStruct((vocab_loc, width), F32),
                jax.ShapeDtypeStruct((toks, width), BF16),
                jax.ShapeDtypeStruct((1, 1), F32),
            ),
            in_specs=[anywhere(), anywhere(), vmem()],
            out_specs=(anywhere(), anywhere(), pl.BlockSpec(memory_space=pltpu.SMEM)),
            scratch_shapes=[
                pltpu.VMEM((depth, nz, chunk, cols), F32), pltpu.VMEM((toks, width), BF16),
                dma(depth), dma(depth, nz), pltpu.SemaphoreType.DMA,
            ],
            compiler_params=pltpu.CompilerParams(vmem_limit_bytes=big),
            name="place",
        )(stack, d_rows, loss)
        return mean_loss.reshape(()), d_rows.reshape(trunk.shape), d_table

    return jax.shard_map(
        per_device,
        mesh=mesh,
        in_specs=(P("tp", None), P("dp", None), P("dp", None), P("dp", None, None)),
        out_specs=(P(), P("dp", None, None), P("tp", None)),
        check_vma=False,
    )
```

time: 645 us -> 618 us (0.958)
  Pallas kernels: 613 us -> 594 us
    pallas_call x3 -> x2, Pallas kernels: 511 us -> 491 us  [the longest x1 452 us: per_device(): pl.pallas_call(functools.partial(finish_kernel, nz, stride, vocab_loc, to...]
where the time goes in v2:
time: 618 us; the launch traced here: 617 us
  Pallas kernels  594 us (96%)
  local copies, waits for them, and re-layouts  19.7 us (3%)
    pallas_call x1, Pallas kernels, per_device(): pl.pallas_call(functools.partial(finish_kernel, nz, stride, vocab_loc, to...  452 us
    pallas_call x1, Pallas kernels, per_device(): pl.pallas_call(functools.partial(token_kernel, nz, tok_total, token_plan)...  103 us
    pallas_call x1, Pallas kernels, per_device(): pl.pallas_call(functools.partial(place_kernel, chunk, tok_total), out_sha...  39.3 us
    gather x1, local copies, waits for them, and re-layouts, per_device(): part = jnp.take(table, local_ids, axis=0, mode='clip')  17 us

profile of v2, /device:TPU:1, one launch (start us, length us, event | category | flops | bytes accessed | tf_op | source)
XLA Modules:
  0.0 617.4 jit_solution(4895172429169178028)
XLA Ops:
  0.6 0.7 fusion
  1.3 0.1 select_n.24
  1.4 0.1 select_n.26
  1.5 0.7 pad_maximum_fusion.ids
  2.2 1.3 fusion.2
  3.5 0.9 copy.9.marks
  4.4 1.7 dynamic-slice_bitcast_fusion.trunk
  6.1 17.0 %gather_fusion = bf16[512,2048]{1,0:T(8,128)(2,1)} fusion(bf16[6288,2048]{1,0:T(8,128)(2,1)} %table.3, s32[1024]{0:T(1024)S(1)} %pad_clamp_fusion), kind=kCustom, calls=%fused_computation | custom fusion | bytes 4196352 | tf_op jit(solution)/shard_map/jit(_take)/gather | solution.py:798
  23.1 103.2 %token_.1 = (f32[512,2048]{1,0:T(8,128)}, f32[4,8,64,2048]{3,2,1,0:T(8,128)}, f32[64,2048]{1,0:T(8,128)}, f32[64,128]{1,0:T(8,128)}, f32[4,8,512]{2,1,0:T(8,128)}, /*index=5*/f32[4,8,128]{2,1,0:T(8,128)}) custom-call(bf16[6288,2048]{1,0:T(8,128)(2,1)} %table.3, bf16[512,2048]{1,0:T(8,128)(2,1)} %gather_fusion, ...), custom_call_target="tpu_custom_call" | custom-call | tf_op jit(solution)/shard_map/token/pallas_call | solution.py:817
  126.3 451.7 %finish.1 = (bf16[512,2048]{1,0:T(8,128)(2,1)}, f32[8,128]{1,0:T(8,128)}, f32[8,4,1584,256]{3,2,1,0:T(8,128)}, f32[8,4,512,256]{3,2,1,0:T(8,128)}) custom-call(bf16[6288,2048]{1,0:T(8,128)(2,1)} %table.3, f32[4,512,2048]{2,1,0:T(8,128)} %bitcast.9, f32[4,8,512]{2,1,0:T(8,128)} %get-tuple-element.16.stats, f32[512,2048]{1,0:T(8,128)} %get-tuple-element.17.du, ...), custom_call_target="tpu_custom_call" | custom-call | tf_op jit(solution)/shard_map/finish/pallas_call | solution.py:860
  578.0 39.3 %place.1 = (f32[6288,2048]{1,0:T(8,128)}, bf16[512,2048]{1,0:T(8,128)(2,1)}, f32[1,1]{1,0:T(1,128)}) custom-call(f32[8,4,1584,256]{3,2,1,0:T(8,128)} %get-tuple-element.21.stack, bf16[512,2048]{1,0:T(8,128)(2,1)} %get-tuple-element.22.rows_in, f32[8,128]{1,0:T(8,128)} %get-tuple-element.23.loss_in), custom_call_target="tpu_custom_call" | custom-call | tf_op jit(solution)/shard_map/place/pallas_call | solution.py:892
  (2 shorter events, 0.0 us)

commit v3 on v2

--- a/solution.py
+++ b/solution.py
@@ -13,7 +13,7 @@
 F32, BF16 = jnp.float32, jnp.bfloat16
 NY, NTP, NX = 4, 8, 4
 WAYS = (1, -1)
-PACE = ((10, 0), (20, 15), (20, 26))
+BESIDE = ((0, 2, 1), (6, 1, 2), (13, 2, 2), (20, 1, 3), (26, 2, 3))
 SHARES = (0.55, 0.55, 0.7)
 ALL = Ellipsis
 NEG = float(jnp.finfo(jnp.float32).min)
@@ -218,20 +218,23 @@
 
 def token_kernel(
     nz, tok_total, plan, table, part, trunk, marks, lab_row, ids,
-    du, ub_all, u_out, r_out, stats, tiles,
-    table_v, ub_v, z_v, run, mine, theirs, row_out, row_in, tile_out, tile_in, pb, rl, fin, land,
+    grads, ub_all, u_out, r_out, stats, tiles,
+    du, trunk_v, grad_v, table_v, ub_v, z_v, run, mine, theirs, row_out, row_in, tile_out, tile_in, pb, rl, fin, land,
     load_sem, part_sem, st_send, st_recv, row_send, row_recv, t_send, t_recv, rs_send, rs_recv, x_send, x_recv,
+    grad_sem,
 ):
     at = Place(nz)
     rows, width = table_v.shape
     toks = ub_v.shape[0]
-    own = trunk.shape[0]
+    own = trunk_v.shape[0]
     steps = z_v.shape[0]
     whole = rows // VT
     tail = rows - whole * VT
 
     part_copy = pltpu.make_async_copy(part, ub_v, part_sem)
     part_copy.start()
+    trunk_copy = pltpu.make_async_copy(trunk.at[pl.ds(pl.multiple_of(at.tp * own, own), own)], trunk_v, grad_sem.at[0])
+    trunk_copy.start()
 
     def load(i):
         start = pl.multiple_of(i * VT, 16)
@@ -251,7 +254,8 @@
     sums.begin()
     sums.pass_on()
     sums.join()
-    hidden = sums.result() + trunk[ALL].astype(F32)
+    trunk_copy.wait()
+    hidden = sums.result() + trunk_v[ALL].astype(F32)
     centered = hidden - jnp.mean(hidden, axis=-1, keepdims=True)
     inv_std = lax.rsqrt(jnp.mean(centered * centered, axis=-1, keepdims=True) + LN_EPS)
     normed = centered * inv_std
@@ -274,12 +278,12 @@
     pace = own / 7.5
     for e in [e for e in spread.events if e not in near]:
         due = max(0, int((e[-1] - near[-1][-1]) / pace)) + 2
-        groups.setdefault(due if due <= steps else max(steps, due - 5), []).append(e)
-    late = [e for due in sorted(groups) if due >= 2 * steps for e in groups[due]]
+        groups.setdefault(due, []).append(e)
+    middle, late = ([e for due in sorted(groups) if (due >= steps) and (due < steps + 6) == m for e in groups[due]] for m in (True, False))
 
     def attend(step):
         for due, events in groups.items():
-            if due < 2 * steps:
+            if due < steps:
 
                 @pl.when(step == due)
                 def _(events=events):
@@ -337,6 +341,7 @@
         stat.append(rdma(mine, theirs.at[i], st_send.at[i], st_recv.at[i], to_tp(rem(at.tp + i, NTP))))
         stat[-1].start()
     theirs[0] = mine[ALL]
+    spread.run(middle)
     for copy in stat:
         copy.wait_recv()
     parts = [theirs[rem(at.tp - j + NTP, NTP)] for j in range(NTP)]
@@ -358,25 +363,29 @@
     for copy in rows_sent:
         copy.start()
     run[0] = jnp.transpose(jnp.broadcast_to(lse, (128, toks)))
-    wide = min(512, width)
     inv_total = 1.0 / tok_total
-    du[ALL] = jnp.zeros(du.shape, F32)
+
+    def put(i):
+        half = rem(i, 2)
+        return pltpu.make_async_copy(grad_v.at[half], grads.at[i], grad_sem.at[half])
 
     def backward(i, carry):
-        attend(i + steps)
         start = start_of(i)
         shift = jnp.concatenate([run[0]] * (VT // 128), axis=1)
         prob = jnp.exp(z_v[i] - shift)
         hit = (lane + start == marks[:, 0:1]) & (lane >= i * VT - start)
-        grad = ((prob - jnp.where(hit, 1.0, 0.0)) * inv_total).astype(BF16)
-        for n in range(width // wide):
-            cols = pl.ds(n * wide, wide)
-            du[:, cols] = du[:, cols] + lax.dot_general(
-                grad, table_v[pl.ds(start, VT), cols], NN_DIMS, preferred_element_type=F32
-            )
+
+        @pl.when(i >= 2)
+        def _():
+            put(i - 2).wait()
+
+        grad_v[rem(i, 2)] = ((prob - jnp.where(hit, 1.0, 0.0)) * inv_total).astype(BF16)
+        put(i).start()
         return carry
 
     lax.fori_loop(0, steps, backward, 0)
+    for i in range(max(0, steps - 2), steps):
+        put(jnp.int32(i)).wait()
     spread.run(late)
     for e in spread.events:
         if e not in near:
@@ -444,45 +453,61 @@
 
 def finish_kernel(
     nz, stride, vocab_loc, tok_total, row_plan, dh_plan, table_plan, chunks,
-    table, ub, stats, du, u, r, tiles,
+    table, ub, stats, grads, u, r, tiles,
     d_trunk, loss, stack, all_dh,
-    pb, rl, fin, land, all_tiles, table_v, ub_v, stage, grad_v, parts, came, total, dh_v,
+    pb, rl, fin, land, all_tiles, table_v, ub_v, grad_v, parts, came, total, dh_v, du, rows_v, logit_v,
     rs_send, rs_recv, row_send, row_recv, z_send, z_recv, i_send, i_recv, x_send, x_recv, s_send, s_recv, t_send, t_recv,
-    load_sem, stage_sem, dh_sem,
+    load_sem, stage_sem, dh_sem, rows_sem, logit_sem,
 ):
     at = Place(nz)
     own, width = u.shape
     win, cols = total.shape
     toks = stats.shape[2]
     block = nz * own
-    slab = stage.shape[1]
+    slab = 128
     first = pl.multiple_of(at.y * stride, 16)
     load = pltpu.make_async_copy(table.at[pl.ds(first, win)], table_v, load_sem)
 
-    depth, per = stage.shape[0], toks // slab
+    depth, per = 4, toks // slab
     slabs = NY * per
+
+    def staged(slot):
+        return du.at[pl.ds(pl.multiple_of(slot * slab, slab), slab)]
 
     def fill(i):
         rows = pl.ds(pl.multiple_of(rem(i, per) * slab, slab), slab)
-        at_slot = rem(i, depth)
-        return pltpu.make_async_copy(ub.at[lax.div(i, jnp.int32(per)), rows], stage.at[at_slot], stage_sem.at[at_slot])
+        slot = rem(i, depth)
+        return pltpu.make_async_copy(ub.at[lax.div(i, jnp.int32(per)), rows], staged(slot), stage_sem.at[slot])
 
     for i in range(depth):
         fill(jnp.int32(i)).start()
     load.start()
+    steps = grads.shape[0]
+
+    def start_of(i):
+        return pl.multiple_of(jnp.minimum(i * VT, vocab_loc - VT), 16)
+
+    def bring(i):
+        half = rem(i, 2)
+        return [
+            pltpu.make_async_copy(table.at[pl.ds(start_of(i), VT)], rows_v.at[half], rows_sem.at[half]),
+            pltpu.make_async_copy(grads.at[i], logit_v.at[half], logit_sem.at[half]),
+        ]
+
+    for copy in bring(jnp.int32(0)):
+        copy.start()
     greet(
         [to_tp(rem(at.tp + i, NTP)) for i in range(1, NTP)]
         + [to_dp(at.dp_of_z(i)) for i in range(1, nz)]
         + [to_dp(at.dp_of_y(way)) for way in WAYS]
     )
     sum_tp = SumTp(at, du, own, pb, rl, fin, rs_send, rs_recv)
-    sum_tp.begin()
 
     def narrow(n):
         def body(k, carry):
             i = n * per + k
             fill(i).wait()
-            ub_v[pl.ds(pl.multiple_of(i * slab, slab), slab)] = stage[rem(i, depth)].astype(BF16)
+            ub_v[pl.ds(pl.multiple_of(i * slab, slab), slab)] = staged(rem(i, depth))[ALL].astype(BF16)
 
             @pl.when(i + depth < slabs)
             def _():
@@ -493,7 +518,6 @@
         lax.fori_loop(0, per, body, 0)
 
     narrow(0)
-    sum_tp.pass_on()
     load.wait()
 
     inv_total = 1.0 / tok_total
@@ -522,7 +546,10 @@
         lax.fori_loop(0, nz, body, 0)
 
     sums = SumZ(at, parts, came, total, chunks, s_send, s_recv)
-    todo = [(c, s) for _, c, s in sorted((k * s + late, c, s) for s in range(1, sums.last + 1) for c, (k, late) in enumerate(PACE))]
+
+    def sum_step(c, k):
+        if k <= sums.last:
+            sums.run(c, k)
 
     def narrow_next(n):
         @pl.when(n + 1 < NY)
@@ -532,9 +559,39 @@
     logits(*chunks[0], narrow_next)
     head(*chunks[0])
     sums.begin(0)
+    wide = min(512, width)
+    du[ALL] = jnp.zeros(du.shape, F32)
+
+    def backward(i, carry):
+        for copy in bring(i):
+            copy.wait()
+
+        @pl.when(i + 1 < steps)
+        def _():
+            for copy in bring(i + 1):
+                copy.start()
+
+        @pl.when(i == min(5, steps - 1))
+        def _():
+            sum_step(0, 1)
+
+        half = rem(i, 2)
+        for n in range(width // wide):
+            cut = pl.ds(n * wide, wide)
+            du[:, cut] = du[:, cut] + jnp.dot(logit_v[half], rows_v[half, :, cut], preferred_element_type=F32)
+        return carry
+
+    lax.fori_loop(0, steps, backward, 0)
+    sum_tp.begin()
+    sum_step(0, 2)
+    logits(*chunks[1])
+    sum_tp.pass_on()
+    head(*chunks[1])
+    sums.begin(1)
     sum_tp.join()
-    logits(*chunks[1])
-    sums.run(*todo[0])
+    sum_step(0, 3)
+    logits(*chunks[2])
+    head(*chunks[2])
     grad = sum_tp.result()
     normed = u[ALL]
     mean_g = jnp.mean(grad, axis=-1, keepdims=True)
@@ -559,10 +616,9 @@
     mine = pltpu.make_async_copy(land.at[at.tp, :, pl.ds(my_col, cols)], all_dh.at[at.tp, 0, here], load_sem)
     mine.start()
     all_tiles[at.z] = tiles[ALL]
-    head(*chunks[1])
-    sums.begin(1)
-    sums.run(*todo[1])
-    logits(*chunks[2])
+    sums.begin(2)
+    sum_step(1, 1)
+    sum_step(0, 4)
     whole_rows.run(whole_rows.events)
     mine.wait()
     for copy in turned:
@@ -573,8 +629,6 @@
 
     blocks = Spread(at, dh_plan, block, dh_block, x_send, x_recv)
     blocks.begin()
-    head(*chunks[2])
-    sums.begin(2)
 
     pieces = {(0, 0): [(blocks.count, [], 0)]}
     for e in blocks.events:
@@ -600,13 +654,15 @@
         meet(k)
     for i in range(whole_rows.count + 1):
         whole_rows.take(i)
-    d_trunk[ALL] = land[ALL].reshape(d_trunk.shape).astype(BF16)
+    ub_v[0:toks] = land[ALL].reshape(toks, width).astype(BF16)
+    keep_rows = pltpu.make_async_copy(ub_v.at[0:toks], d_trunk, rows_sem.at[0])
+    keep_rows.start()
     upper = lax.broadcasted_iota(jnp.int32, loss.shape, 1) >= 64
     loss[ALL] = sum(
         jnp.where(upper == (z % 2 == 0), all_tiles[z, rem(y - at.y + NY, NY)], 0.0) for z in range(nz) for y in range(NY)
     )
 
-    beside = {at_piece: todo[2 + k] for k, at_piece in enumerate((0, 1, 4, 7, 15, 24)) if 2 + k < len(todo)}
+    beside = {k: (c, step) for k, c, step in BESIDE if step <= sums.last}
     low = (at.tp * vocab_loc + at.y * stride).astype(F32)
 
     def place_of(e):
@@ -675,8 +731,8 @@
         src = dst if any(off) else total.at[pl.ds(lo, hi - lo)]
         return rdma(src, dst, t_send.at[i], t_recv.at[i], device[axis, way])
 
-    for step in todo[2 + len(beside) :]:
-        sums.run(*step)
+    for c in range(1, len(chunks)):
+        sum_step(c, 4)
     for i in sum(starts, []):
         copy_of(i).start()
     keep = pltpu.make_async_copy(total, stack.at[at.z, at.y], load_sem)
@@ -686,6 +742,7 @@
         for j in new:
             copy_of(j).start()
     keep.wait()
+    keep_rows.wait()
     for i in range(len(sends)):
         copy_of(i).wait_send()
     sums.end()
@@ -693,73 +750,73 @@
     blocks.end()
 
 
-def place_kernel(chunk, tok_total, stack, rows_in, loss_in, out, rows_out, loss_out, slots, rows_v, load_sem, store_sem, rows_sem):
+def place_kernel(chunk, tok_total, stack, rows_in, loss_in, out, rows_out, loss_out, slots, rows_v, rest_v, load_sem, store_sem, rows_sem, rest_sem):
     nz, ny, have, cols = stack.shape
     depth = slots.shape[0]
     per = have // chunk
     total = ny * per
     ahead = depth // 2
 
-    def load(i):
+    def loads(i):
         y, row = lax.div(i, jnp.int32(per)), pl.multiple_of(rem(i, per) * chunk, 8)
         s = rem(i, depth)
-        return pltpu.make_async_copy(stack.at[:, y, pl.ds(row, chunk)], slots.at[s], load_sem.at[s])
-
-    def stores(i):
-        s, row = rem(i, depth), pl.multiple_of(i * chunk, 8)
         return [
-            pltpu.make_async_copy(slots.at[s, j], out.at[pl.ds(row, chunk), pl.ds(j * cols, cols)], store_sem.at[s, j])
+            pltpu.make_async_copy(
+                stack.at[j, y, pl.ds(row, chunk)], slots.at[s, :, pl.ds(j * cols, cols)], load_sem.at[s, j]
+            )
             for j in range(nz)
         ]
 
+    def store(i):
+        s, row = rem(i, depth), pl.multiple_of(i * chunk, 8)
+        return pltpu.make_async_copy(slots.at[s], out.at[pl.ds(row, chunk)], store_sem.at[s])
+
     def prime(i, carry):
-        load(i).start()
+        for copy in loads(i):
+            copy.start()
         return carry
 
     def body(i, carry):
-        load(i).wait()
-        for copy in stores(i):
-            copy.start()
+        for copy in loads(i):
+            copy.wait()
+        store(i).start()
 
         @pl.when(i + ahead < total)
         def _():
             @pl.when(i >= ahead)
             def _():
-                for copy in stores(i - ahead):
-                    copy.wait()
-
-            load(i + ahead).start()
+                store(i - ahead).wait()
+
+            for copy in loads(i + ahead):
+                copy.start()
 
         return carry
 
     def drain(i, carry):
-        for copy in stores(i):
-            copy.wait()
+        store(i).wait()
         return carry
 
     rows_load = pltpu.make_async_copy(rows_in, rows_v, rows_sem)
     rows_store = pltpu.make_async_copy(rows_v, rows_out, rows_sem)
     lax.fori_loop(0, ahead, prime, 0)
     rows_load.start()
+    used = per * chunk
+    left = have - used
+    rest = pltpu.make_async_copy(stack.at[:, ny - 1, pl.ds(used, left)], rest_v, rest_sem.at[0])
+    rest.start()
+    tails = [
+        pltpu.make_async_copy(rest_v.at[j], out.at[pl.ds(ny * used, left), pl.ds(j * cols, cols)], rest_sem.at[j])
+        for j in range(nz)
+    ]
     lane = lax.broadcasted_iota(jnp.int32, (1, 128), 1)
     loss_out[0, 0] = jnp.sum(jnp.where(rem(lane, 64) == 0, loss_in[0:1], 0.0)) / tok_total
     rows_load.wait()
     rows_store.start()
+    rest.wait()
+    for copy in tails:
+        copy.start()
     lax.fori_loop(0, total, body, 0)
     lax.fori_loop(total - 2 * ahead, total, drain, 0)
-    used = per * chunk
-    left = have - used
-    rest = pltpu.make_async_copy(stack.at[:, ny - 1, pl.ds(used, left)], slots.at[0, :, pl.ds(0, left)], load_sem.at[0])
-    rest.start()
-    rest.wait()
-    tails = [
-        pltpu.make_async_copy(
-            slots.at[0, j, pl.ds(0, left)], out.at[pl.ds(ny * used, left), pl.ds(j * cols, cols)], store_sem.at[0, j]
-        )
-        for j in range(nz)
-    ]
-    for copy in tails:
-        copy.start()
     for copy in tails:
         copy.wait()
     rows_store.wait()
@@ -775,6 +832,10 @@
 
 def dma(*shape):
     return pltpu.SemaphoreType.DMA(shape)
+
+
+def twice(*shape):
+    return [dma(*shape)] * 2
 
 
 def solution(mesh):
@@ -796,8 +857,8 @@
         row_start = tp * vocab_loc
         local_ids = ids.reshape(toks) - row_start
         part = jnp.take(table, local_ids, axis=0, mode="clip")
-        trunk_own = lax.dynamic_slice_in_dim(trunk.reshape(toks, width), tp * own, own, 0)
-
+
+        tp_sems = twice(10)
         tp_scratch = [
             pltpu.VMEM((4, own, width), F32),
             pltpu.VMEM((2, own // 2, width), F32),
@@ -814,19 +875,22 @@
         steps = pl.cdiv(vocab_loc, VT)
         token_plan = gather_plan((NX, NY), two_colours(0, own, 0.5), 16, hold=2 * own)
         sends = 2 * len(token_plan[0]) + 1
-        du, ub, u_own, r_own, stats, tiles = pl.pallas_call(
+        grads, ub, u_own, r_own, stats, tiles = pl.pallas_call(
             functools.partial(token_kernel, nz, tok_total, token_plan),
             out_shape=(
-                jax.ShapeDtypeStruct((toks, width), F32),
+                jax.ShapeDtypeStruct((steps, toks, VT), BF16),
                 jax.ShapeDtypeStruct((NY, NTP, own, width), F32),
                 jax.ShapeDtypeStruct((own, width), F32),
                 jax.ShapeDtypeStruct((own, 128), F32),
                 jax.ShapeDtypeStruct((NY, 8, toks), F32),
                 jax.ShapeDtypeStruct((NY, 8, 128), F32),
             ),
-            in_specs=[anywhere(), anywhere(), vmem(), vmem(), vmem(), vmem()],
-            out_specs=(vmem(), anywhere(), vmem(), vmem(), vmem(), vmem()),
+            in_specs=[anywhere(), anywhere(), anywhere(), vmem(), vmem(), vmem()],
+            out_specs=(anywhere(), anywhere(), vmem(), vmem(), vmem(), vmem()),
             scratch_shapes=[
+                pltpu.VMEM((toks, width), F32),
+                pltpu.VMEM((own, width), BF16),
+                pltpu.VMEM((2, toks, VT), BF16),
                 pltpu.VMEM((vocab_loc, width), BF16),
                 pltpu.VMEM((toks, width), BF16),
                 pltpu.VMEM((steps, toks, VT), F32),
@@ -838,17 +902,16 @@
                 pltpu.VMEM((8, 128), F32),
                 pltpu.VMEM((NY - 1, 8, 128), F32),
                 *tp_scratch,
-                dma(steps), pltpu.SemaphoreType.DMA, dma(NTP), dma(NTP),
-                dma(NY - 1), dma(NY - 1), dma(NY - 1), dma(NY - 1), dma(10), dma(10), dma(sends), dma(sends),
+                dma(steps), pltpu.SemaphoreType.DMA, *twice(NTP), *twice(NY - 1), *twice(NY - 1), *tp_sems, *twice(sends), dma(2),
             ],
             compiler_params=pltpu.CompilerParams(collective_id=0, has_side_effects=True, vmem_limit_bytes=big),
             name="token",
-        )(table, part, trunk_own, marks, lab_row, ids_tile)
+        )(table, part, trunk.reshape(toks, width), marks, lab_row, ids_tile)
 
         row_plan = gather_plan((NX, 1), two_colours(0, own, 1), 16)
         dh_plan = gather_plan((NX, NY), two_colours(0, block, 0.5), block // 4)
-        lead = 16 * (win // 96)
-        middle = lead + 16 * pl.cdiv(win - lead, 32)
+        lead = 16 * pl.cdiv(win, 48)
+        middle = 2 * lead
         chunks = ((0, lead), (lead, middle), (middle, win))
         third = 8 * pl.cdiv(win, 24)
         table_chunks = ((0, third), (third, 2 * third), (2 * third, win))
@@ -867,28 +930,29 @@
                 jax.ShapeDtypeStruct((nz, NY, win, cols), F32),
                 jax.ShapeDtypeStruct((NTP, NY, block, cols), F32),
             ),
-            in_specs=[anywhere(), anywhere(), vmem(), vmem(), vmem(), vmem(), vmem()],
-            out_specs=(vmem(), vmem(), anywhere(), anywhere()),
+            in_specs=[anywhere(), anywhere(), vmem(), anywhere(), vmem(), vmem(), vmem()],
+            out_specs=(anywhere(), vmem(), anywhere(), anywhere()),
             scratch_shapes=[
                 *tp_scratch,
                 pltpu.VMEM((nz, NY, 8, 128), F32),
                 pltpu.VMEM((win, width), BF16),
                 pltpu.VMEM((NY * toks, width), BF16),
-                pltpu.VMEM((4, 128, width), F32),
                 pltpu.VMEM((middle - lead, NY * toks), BF16),
                 pltpu.VMEM((nz, win, cols), F32),
                 pltpu.VMEM((nz - 1, win, cols), F32),
                 pltpu.VMEM((win, cols), F32),
                 pltpu.VMEM((2, block, cols), F32),
-                dma(10), dma(10), dma(counts[0]), dma(counts[0]), dma(nz), dma(nz), dma(nz), dma(nz),
-                dma(counts[1]), dma(counts[1]), dma(*zs), dma(*zs), dma(counts[2]), dma(counts[2]),
-                pltpu.SemaphoreType.DMA, dma(4), dma(2),
+                pltpu.VMEM((toks, width), F32),
+                pltpu.VMEM((2, VT, width), BF16),
+                pltpu.VMEM((2, toks, VT), BF16),
+                *tp_sems, *twice(counts[0]), *twice(nz), *twice(nz), *twice(counts[1]), *twice(*zs), *twice(counts[2]),
+                pltpu.SemaphoreType.DMA, dma(4), *twice(2), dma(2),
             ],
             compiler_params=pltpu.CompilerParams(collective_id=1, has_side_effects=True, vmem_limit_bytes=67_000_000),
             name="finish",
-        )(table, ub.reshape(NY, toks, width), stats, du, u_own, r_own, tiles)
-        depth = 8
-        chunk = next(n for n in range(224, 0, -8) if stride % n == 0 and NY * stride >= n * depth)
+        )(table, ub.reshape(NY, toks, width), stats, grads, u_own, r_own, tiles)
+        depth = 16 if nz == 8 else 8
+        chunk = next(n for n in range(112, 0, -8) if stride % n == 0 and NY * stride >= n * depth)
         d_table, d_rows, mean_loss = pl.pallas_call(
             functools.partial(place_kernel, chunk, tok_total),
             out_shape=(
@@ -899,8 +963,8 @@
             in_specs=[anywhere(), anywhere(), vmem()],
             out_specs=(anywhere(), anywhere(), pl.BlockSpec(memory_space=pltpu.SMEM)),
             scratch_shapes=[
-                pltpu.VMEM((depth, nz, chunk, cols), F32), pltpu.VMEM((toks, width), BF16),
-                dma(depth), dma(depth, nz), pltpu.SemaphoreType.DMA,
+                pltpu.VMEM((depth, chunk, width), F32), pltpu.VMEM((toks, width), BF16),
+                pltpu.VMEM((nz, win - stride, cols), F32), dma(depth, nz), dma(depth), pltpu.SemaphoreType.DMA, dma(nz),
             ],
             compiler_params=pltpu.CompilerParams(vmem_limit_bytes=big),
             name="place",

time: 618 us -> 600 us (0.971)
  Pallas kernels: 594 us -> 577 us
    pallas_call x1, Pallas kernels: 103 us -> 88.8 us  [per_device(): pl.pallas_call(functools.partial(token_kernel, nz, tok_total, token_plan)...]
where the time goes in v3:
time: 600 us; the launch traced here: 599 us
  Pallas kernels  577 us (96%)
  local copies, waits for them, and re-layouts  18.1 us (3%)
    pallas_call x1, Pallas kernels, per_device(): pl.pallas_call(functools.partial(finish_kernel, nz, stride, vocab_loc, to...  450 us
    pallas_call x1, Pallas kernels, per_device(): pl.pallas_call(functools.partial(token_kernel, nz, tok_total, token_plan)...  88.8 us
    pallas_call x1, Pallas kernels, per_device(): pl.pallas_call(functools.partial(place_kernel, chunk, tok_total), out_sha...  38.1 us
    gather x1, local copies, waits for them, and re-layouts, per_device(): part = jnp.take(table, local_ids, axis=0, mode='clip')  17 us

profile of v3, /device:TPU:1, one launch (start us, length us, event | category | flops | bytes accessed | tf_op | source)
XLA Modules:
  0.0 598.9 jit_solution(12403967145453806847)
XLA Ops:
  0.6 0.7 fusion
  1.3 0.1 select_n.20
  1.4 0.1 select_n.22
  1.5 0.7 pad_maximum_fusion.ids
  2.2 1.3 fusion.2
  3.5 0.9 copy.9.marks
  4.4 17.0 %gather_fusion = bf16[512,2048]{1,0:T(8,128)(2,1)} fusion(bf16[6288,2048]{1,0:T(8,128)(2,1)} %table.3, s32[1024]{0:T(1024)S(1)} %pad_clamp_fusion), kind=kCustom, calls=%fused_computation | custom fusion | bytes 4196352 | tf_op jit(solution)/shard_map/jit(_take)/gather | solution.py:859
  21.4 88.8 %token_.1 = (bf16[13,512,512]{2,1,0:T(8,128)(2,1)}, f32[4,8,64,2048]{3,2,1,0:T(8,128)}, f32[64,2048]{1,0:T(8,128)}, f32[64,128]{1,0:T(8,128)}, f32[4,8,512]{2,1,0:T(8,128)}, /*index=5*/f32[4,8,128]{2,1,0:T(8,128)}) custom-call(bf16[6288,2048]{1,0:T(8,128)(2,1)} %table.3, bf16[512,2048]{1,0:T(8,128)(2,1)} %gather_fusion, bf16[512,2048]{1,0:T(8,128)(2,1)} %bitcast.9, ...), custom_call_target="tpu_custom_call" | custom-call | tf_op jit(solution)/shard_map/token/pallas_call | solution.py:878
  110.3 450.4 %finish.1 = (bf16[512,2048]{1,0:T(8,128)(2,1)}, f32[8,128]{1,0:T(8,128)}, f32[8,4,1584,256]{3,2,1,0:T(8,128)}, f32[8,4,512,256]{3,2,1,0:T(8,128)}) custom-call(bf16[6288,2048]{1,0:T(8,128)(2,1)} %table.3, f32[4,512,2048]{2,1,0:T(8,128)} %bitcast.8, f32[4,8,512]{2,1,0:T(8,128)} %get-tuple-element.16.stats, bf16[13,512,512]{2,1,0:T(8,128)(2,1)} %get-tuple-element.17.grads, ...), custom_call_target="tpu_custom_call" | custom-call | tf_op jit(solution)/shard_map/finish/pallas_call | solution.py:923
  560.6 38.1 %place.1 = (f32[6288,2048]{1,0:T(8,128)}, bf16[512,2048]{1,0:T(8,128)(2,1)}, f32[1,1]{1,0:T(1,128)}) custom-call(f32[8,4,1584,256]{3,2,1,0:T(8,128)} %get-tuple-element.21.stack, bf16[512,2048]{1,0:T(8,128)(2,1)} %get-tuple-element.22.rows_in, f32[8,128]{1,0:T(8,128)} %get-tuple-element.23.loss_in), custom_call_target="tpu_custom_call" | custom-call | tf_op jit(solution)/shard_map/place/pallas_call | solution.py:956
  (2 shorter events, 0.0 us)

commit v4 on v3

--- a/solution.py
+++ b/solution.py
@@ -13,6 +13,8 @@
 F32, BF16 = jnp.float32, jnp.bfloat16
 NY, NTP, NX = 4, 8, 4
 WAYS = (1, -1)
+SUB = 8
+LANES = 128
 BESIDE = ((0, 2, 1), (6, 1, 2), (13, 2, 2), (20, 1, 3), (26, 2, 3))
 SHARES = (0.55, 0.55, 0.7)
 ALL = Ellipsis
@@ -49,6 +51,10 @@
         return rem(self.z + step + self.nz, self.nz) * NY + self.y
 
 
+def repeat(count, body):
+    lax.fori_loop(0, count, body, 0)
+
+
 def to_tp(tp):
     return {"tp": tp}
 
@@ -67,7 +73,7 @@
     barrier = pltpu.get_barrier_semaphore()
     for device in devices:
         pl.semaphore_signal(barrier, inc=1, device_id=device, device_id_type=MESH)
-    pl.semaphore_wait(barrier, len(devices))
+    return lambda: pl.semaphore_wait(barrier, len(devices))
 
 
 class SumTp:
@@ -110,7 +116,7 @@
             self.copies[4 + h].wait_recv()
             rows = pl.ds(h * self.half, self.half)
             self.pb[1 + h, rows] = self.pb[1 + h, rows] + self.rl[h]
-            self.copy(8 + h, self.part(1 + h, h), self.fin.at[2 + h], tp).start()
+            self.copy(SUB + h, self.part(1 + h, h), self.fin.at[2 + h], tp).start()
         self.merge(3)
 
     def result(self):
@@ -140,7 +146,7 @@
         if gone > last:
             return []
         if gone == last:
-            mid = lo + 8 * pl.cdiv(hi - lo, 16)
+            mid = lo + SUB * pl.cdiv(hi - lo, 16)
             lo, hi = (lo, mid) if way > 0 else (mid, hi)
         return [] if lo == hi else [post(axis, way, off, lo, hi, order, now)]
 
@@ -164,7 +170,7 @@
 
 
 def two_colours(lo, hi, share, now=0):
-    split = lo + 8 * round((hi - lo) * share / 8)
+    split = lo + SUB * round((hi - lo) * share / SUB)
     return [(lo, split, (0, 1), now), (split, hi, (1, 0), now)]
 
 
@@ -243,14 +249,14 @@
     tail_copy = pltpu.make_async_copy(
         table.at[pl.ds(whole * VT, tail)], table_v.at[pl.ds(whole * VT, tail)], load_sem.at[whole]
     )
-    greet([to_tp(rem(at.tp + i, NTP)) for i in range(1, NTP)] + [to_dp(at.dp_of_y(i)) for i in range(1, NY)])
+    met_all = greet([to_tp(rem(at.tp + i, NTP)) for i in range(1, NTP)] + [to_dp(at.dp_of_y(i)) for i in range(1, NY)])
     part_copy.wait()
     for i in range(whole):
         load(i).start()
     tail_copy.start()
-    mine_only = (marks[:, 1:2] >= 0) & (marks[:, 1:2] < rows)
-    du[ALL] = jnp.where(mine_only, ub_v[ALL].astype(F32), 0.0)
+    du[ALL] = ub_v[ALL].astype(F32)
     sums = SumTp(at, du, own, pb, rl, fin, rs_send, rs_recv)
+    met_all()
     sums.begin()
     sums.pass_on()
     sums.join()
@@ -300,7 +306,7 @@
         return pl.multiple_of(jnp.minimum(i * VT, rows - VT), 16)
 
     def fold(op, v):
-        return functools.reduce(op, [v[:, j : j + 128] for j in range(0, VT, 128)])
+        return functools.reduce(op, [v[:, j : j + LANES] for j in range(0, VT, LANES)])
 
     def forward(i, carry):
         attend(i)
@@ -322,7 +328,7 @@
         run[1] = run[1] + fold(jnp.add, jnp.where(hit, z, 0.0))
         return carry
 
-    lax.fori_loop(0, steps, forward, 0)
+    repeat(steps, forward)
     top = jnp.max(run[0], axis=1, keepdims=True)
     run[0] = jnp.zeros(run.shape[1:], F32)
 
@@ -330,12 +336,12 @@
         run[0] = run[0] + fold(jnp.add, jnp.exp(z_v[i] - top))
         return carry
 
-    lax.fori_loop(0, steps, exps, 0)
+    repeat(steps, exps)
     total = jnp.sum(run[0], axis=1, keepdims=True)
     label = jnp.sum(run[1], axis=1, keepdims=True)
-    narrow = lax.broadcasted_iota(jnp.int32, (toks, 128), 1)
+    narrow = lax.broadcasted_iota(jnp.int32, (toks, LANES), 1)
     packed = jnp.where(narrow == 0, top, jnp.where(narrow == 1, total, jnp.where(narrow == 2, label, 0.0)))
-    mine[ALL] = jnp.transpose(packed)[:8]
+    mine[ALL] = jnp.transpose(packed)[:SUB]
     stat = []
     for i in range(1, NTP):
         stat.append(rdma(mine, theirs.at[i], st_send.at[i], st_recv.at[i], to_tp(rem(at.tp + i, NTP))))
@@ -350,7 +356,7 @@
     label = functools.reduce(jnp.add, [p[2:3] for p in parts])
     lse = peak + jnp.log(total)
     loss = jnp.sum(jnp.log(total) + peak - label, axis=1, keepdims=True)
-    sub = lax.broadcasted_iota(jnp.int32, (8, toks), 0)
+    sub = lax.broadcasted_iota(jnp.int32, (SUB, toks), 0)
     row_out[ALL] = jnp.where(sub == 0, lse, jnp.where(sub == 1, lab_row[ALL], 0.0))
     upper = lax.broadcasted_iota(jnp.int32, ids.shape, 1) >= 64
     tile_out[ALL] = jnp.where(upper == (rem(at.z, 2) == 1), ids[ALL], loss)
@@ -362,7 +368,7 @@
         rows_sent.append(rdma(tile_out, tile_in.at[i], t_send.at[i], t_recv.at[i], to_y))
     for copy in rows_sent:
         copy.start()
-    run[0] = jnp.transpose(jnp.broadcast_to(lse, (128, toks)))
+    run[0] = jnp.transpose(jnp.broadcast_to(lse, (LANES, toks)))
     inv_total = 1.0 / tok_total
 
     def put(i):
@@ -371,7 +377,7 @@
 
     def backward(i, carry):
         start = start_of(i)
-        shift = jnp.concatenate([run[0]] * (VT // 128), axis=1)
+        shift = jnp.concatenate([run[0]] * (VT // LANES), axis=1)
         prob = jnp.exp(z_v[i] - shift)
         hit = (lane + start == marks[:, 0:1]) & (lane >= i * VT - start)
 
@@ -383,7 +389,7 @@
         put(i).start()
         return carry
 
-    lax.fori_loop(0, steps, backward, 0)
+    repeat(steps, backward)
     for i in range(max(0, steps - 2), steps):
         put(jnp.int32(i)).wait()
     spread.run(late)
@@ -411,7 +417,7 @@
     def rows(self, c, s, way):
         lo, hi = self.chunks[c]
         if s == 1:
-            mid = lo + 8 * pl.cdiv(hi - lo, 16)
+            mid = lo + SUB * pl.cdiv(hi - lo, 16)
             lo, hi = (lo, mid) if way > 0 else (mid, hi)
         return pl.ds(lo, hi - lo)
 
@@ -464,9 +470,12 @@
     win, cols = total.shape
     toks = stats.shape[2]
     block = nz * own
-    slab = 128
+    slab = LANES
     first = pl.multiple_of(at.y * stride, 16)
-    load = pltpu.make_async_copy(table.at[pl.ds(first, win)], table_v, load_sem)
+    loads = [
+        pltpu.make_async_copy(table.at[pl.ds(first + lo, hi - lo)], table_v.at[lo:hi], copy_sem)
+        for (lo, hi), copy_sem in zip(chunks, (load_sem, dh_sem.at[0], dh_sem.at[1]))
+    ]
 
     depth, per = 4, toks // slab
     slabs = NY * per
@@ -479,9 +488,9 @@
         slot = rem(i, depth)
         return pltpu.make_async_copy(ub.at[lax.div(i, jnp.int32(per)), rows], staged(slot), stage_sem.at[slot])
 
+    loads[0].start()
     for i in range(depth):
         fill(jnp.int32(i)).start()
-    load.start()
     steps = grads.shape[0]
 
     def start_of(i):
@@ -494,9 +503,9 @@
             pltpu.make_async_copy(grads.at[i], logit_v.at[half], logit_sem.at[half]),
         ]
 
-    for copy in bring(jnp.int32(0)):
+    for copy in loads[1:] + bring(jnp.int32(0)):
         copy.start()
-    greet(
+    met_all = greet(
         [to_tp(rem(at.tp + i, NTP)) for i in range(1, NTP)]
         + [to_dp(at.dp_of_z(i)) for i in range(1, nz)]
         + [to_dp(at.dp_of_y(way)) for way in WAYS]
@@ -515,10 +524,10 @@
 
             return carry
 
-        lax.fori_loop(0, per, body, 0)
-
+        repeat(per, body)
+
+    loads[0].wait()
     narrow(0)
-    load.wait()
 
     inv_total = 1.0 / tok_total
 
@@ -527,7 +536,7 @@
 
         def body(n, carry):
             ahead(n)
-            cut = pl.ds(pl.multiple_of(n * toks, 128), toks)
+            cut = pl.ds(pl.multiple_of(n * toks, LANES), toks)
             z = lax.dot_general(table_v[lo:hi, :], ub_v[cut, :], NT_DIMS, preferred_element_type=F32)
             row = stats[n]
             prob = jnp.exp(z - row[0:1])
@@ -535,15 +544,15 @@
             grad_v[0 : hi - lo, cut] = ((prob - jnp.where(hit, 1.0, 0.0)) * inv_total).astype(BF16)
             return carry
 
-        lax.fori_loop(0, NY, body, 0)
+        repeat(NY, body)
 
     def head(lo, hi):
         def body(n, carry):
-            cut = pl.ds(pl.multiple_of(n * cols, 128), cols)
+            cut = pl.ds(pl.multiple_of(n * cols, LANES), cols)
             parts[n, lo:hi] = jnp.dot(grad_v[0 : hi - lo, :], ub_v[:, cut], preferred_element_type=F32)
             return carry
 
-        lax.fori_loop(0, nz, body, 0)
+        repeat(nz, body)
 
     sums = SumZ(at, parts, came, total, chunks, s_send, s_recv)
 
@@ -558,7 +567,14 @@
 
     logits(*chunks[0], narrow_next)
     head(*chunks[0])
+    met_all()
     sums.begin(0)
+    known = [
+        rdma(tiles, all_tiles.at[at.z], i_send.at[i], i_recv.at[i], to_dp(at.dp_of_z(i))) for i in range(1, nz)
+    ]
+    for copy in known:
+        copy.start()
+    all_tiles[at.z] = tiles[ALL]
     wide = min(512, width)
     du[ALL] = jnp.zeros(du.shape, F32)
 
@@ -581,9 +597,11 @@
             du[:, cut] = du[:, cut] + jnp.dot(logit_v[half], rows_v[half, :, cut], preferred_element_type=F32)
         return carry
 
-    lax.fori_loop(0, steps, backward, 0)
+    repeat(steps, backward)
     sum_tp.begin()
     sum_step(0, 2)
+    for copy in loads[1:]:
+        copy.wait()
     logits(*chunks[1])
     sum_tp.pass_on()
     head(*chunks[1])
@@ -606,22 +624,20 @@
     here = pl.ds(pl.multiple_of(at.z * own, own), own)
     turned = []
     for i in range(1, nz):
-        col, to_z = pl.multiple_of(rem(at.z + i, nz) * cols, 128), to_dp(at.dp_of_z(i))
+        col, to_z = pl.multiple_of(rem(at.z + i, nz) * cols, LANES), to_dp(at.dp_of_z(i))
         src = land.at[at.tp, :, pl.ds(col, cols)]
         turned.append(rdma(src, all_dh.at[at.tp, 0, here], z_send.at[i], z_recv.at[i], to_z))
-        turned.append(rdma(tiles, all_tiles.at[at.z], i_send.at[i], i_recv.at[i], to_z))
     for copy in turned:
         copy.start()
-    my_col = pl.multiple_of(at.z * cols, 128)
+    my_col = pl.multiple_of(at.z * cols, LANES)
     mine = pltpu.make_async_copy(land.at[at.tp, :, pl.ds(my_col, cols)], all_dh.at[at.tp, 0, here], load_sem)
     mine.start()
-    all_tiles[at.z] = tiles[ALL]
     sums.begin(2)
     sum_step(1, 1)
     sum_step(0, 4)
     whole_rows.run(whole_rows.events)
     mine.wait()
-    for copy in turned:
+    for copy in turned + known:
         copy.wait_recv()
 
     def dh_block(dx, dy, cross, lo, hi):
@@ -716,8 +732,8 @@
         return carry
 
     fetch(jnp.int32(0)).start()
-    lax.fori_loop(0, len(order), piece, 0)
-    for copy in turned:
+    repeat(len(order), piece)
+    for copy in turned + known:
         copy.wait_send()
 
     sends, starts, events = table_plan
@@ -750,6 +766,38 @@
     blocks.end()
 
 
+def pick_kernel(group, table, marks, out, eights, sem):
+    toks = out.shape[0]
+    rows = table.shape[0]
+    block = 32
+
+    def fetch(t, carry):
+        eight = pl.multiple_of(group[t] * SUB, SUB)
+        mine = eights.at[pl.ds(pl.multiple_of(t * SUB, SUB), SUB)]
+        pltpu.make_async_copy(table.at[pl.ds(eight, SUB)], mine, sem.at[lax.div(t, jnp.int32(part))]).start()
+        return carry
+
+    part = toks // sem.shape[0]
+    lax.fori_loop(0, toks, fetch, 0, unroll=SUB)
+    lane = lax.broadcasted_iota(jnp.int32, (block, SUB * block), 1)
+    first = SUB * lax.broadcasted_iota(jnp.int32, (block, SUB * block), 0)
+
+    def choose(b, carry):
+        at = pl.multiple_of(b * block, block)
+        row = marks[pl.ds(at, block), 1:2]
+        hit = (lane - first == rem(row, SUB)) & (row >= 0) & (row < rows)
+        some = eights[pl.ds(pl.multiple_of(at * SUB, SUB), SUB * block), :]
+        out[pl.ds(at, block)] = jnp.dot(
+            jnp.where(hit, 1.0, 0.0).astype(BF16), some, preferred_element_type=F32
+        ).astype(BF16)
+        return carry
+
+    for q in range(sem.shape[0]):
+        whole = pl.ds(q * part * SUB, part * SUB)
+        pltpu.make_async_copy(table.at[pl.ds(0, part * SUB)], eights.at[whole], sem.at[q]).wait()
+        lax.fori_loop(q * part // block, (q + 1) * part // block, choose, 0)
+
+
 def place_kernel(chunk, tok_total, stack, rows_in, loss_in, out, rows_out, loss_out, slots, rows_v, rest_v, load_sem, store_sem, rows_sem, rest_sem):
     nz, ny, have, cols = stack.shape
     depth = slots.shape[0]
@@ -758,7 +806,7 @@
     ahead = depth // 2
 
     def loads(i):
-        y, row = lax.div(i, jnp.int32(per)), pl.multiple_of(rem(i, per) * chunk, 8)
+        y, row = lax.div(i, jnp.int32(per)), pl.multiple_of(rem(i, per) * chunk, SUB)
         s = rem(i, depth)
         return [
             pltpu.make_async_copy(
@@ -768,7 +816,7 @@
         ]
 
     def store(i):
-        s, row = rem(i, depth), pl.multiple_of(i * chunk, 8)
+        s, row = rem(i, depth), pl.multiple_of(i * chunk, SUB)
         return pltpu.make_async_copy(slots.at[s], out.at[pl.ds(row, chunk)], store_sem.at[s])
 
     def prime(i, carry):
@@ -798,7 +846,7 @@
 
     rows_load = pltpu.make_async_copy(rows_in, rows_v, rows_sem)
     rows_store = pltpu.make_async_copy(rows_v, rows_out, rows_sem)
-    lax.fori_loop(0, ahead, prime, 0)
+    repeat(ahead, prime)
     rows_load.start()
     used = per * chunk
     left = have - used
@@ -808,14 +856,14 @@
         pltpu.make_async_copy(rest_v.at[j], out.at[pl.ds(ny * used, left), pl.ds(j * cols, cols)], rest_sem.at[j])
         for j in range(nz)
     ]
-    lane = lax.broadcasted_iota(jnp.int32, (1, 128), 1)
+    lane = lax.broadcasted_iota(jnp.int32, (1, LANES), 1)
     loss_out[0, 0] = jnp.sum(jnp.where(rem(lane, 64) == 0, loss_in[0:1], 0.0)) / tok_total
     rows_load.wait()
     rows_store.start()
     rest.wait()
     for copy in tails:
         copy.start()
-    lax.fori_loop(0, total, body, 0)
+    repeat(total, body)
     lax.fori_loop(total - 2 * ahead, total, drain, 0)
     for copy in tails:
         copy.wait()
@@ -856,7 +904,7 @@
         dp, tp = lax.axis_index("dp"), lax.axis_index("tp")
         row_start = tp * vocab_loc
         local_ids = ids.reshape(toks) - row_start
-        part = jnp.take(table, local_ids, axis=0, mode="clip")
+        owned = (local_ids >= 0) & (local_ids < vocab_loc)
 
         tp_sems = twice(10)
         tp_scratch = [
@@ -868,10 +916,19 @@
         ids_f = ids.reshape(NTP, own).astype(F32)
         blank = jnp.zeros_like(ids_f)
         even = rem(lax.div(dp, jnp.int32(NY)), 2) == 0
-        pad = ((0, 0), (0, 128 - 2 * own))
+        pad = ((0, 0), (0, LANES - 2 * own))
         ids_tile = jnp.pad(jnp.concatenate([jnp.where(even, ids_f, blank), jnp.where(even, blank, ids_f)], axis=1), pad)
         marks = jnp.stack([labels.reshape(toks) - row_start, local_ids], axis=1)
         lab_row = labels.reshape(1, toks).astype(F32)
+        part = pl.pallas_call(
+            pick_kernel,
+            out_shape=jax.ShapeDtypeStruct((toks, width), BF16),
+            in_specs=[pl.BlockSpec(memory_space=pltpu.SMEM), anywhere(), vmem()],
+            out_specs=vmem(),
+            scratch_shapes=[pltpu.VMEM((SUB * toks, width), BF16), dma(SUB)],
+            compiler_params=pltpu.CompilerParams(vmem_limit_bytes=big),
+            name="pick",
+        )(jnp.where(owned, local_ids // SUB, jnp.arange(toks)), table, marks)
         steps = pl.cdiv(vocab_loc, VT)
         token_plan = gather_plan((NX, NY), two_colours(0, own, 0.5), 16, hold=2 * own)
         sends = 2 * len(token_plan[0]) + 1
@@ -881,9 +938,9 @@
                 jax.ShapeDtypeStruct((steps, toks, VT), BF16),
                 jax.ShapeDtypeStruct((NY, NTP, own, width), F32),
                 jax.ShapeDtypeStruct((own, width), F32),
-                jax.ShapeDtypeStruct((own, 128), F32),
-                jax.ShapeDtypeStruct((NY, 8, toks), F32),
-                jax.ShapeDtypeStruct((NY, 8, 128), F32),
+                jax.ShapeDtypeStruct((own, LANES), F32),
+                jax.ShapeDtypeStruct((NY, SUB, toks), F32),
+                jax.ShapeDtypeStruct((NY, SUB, LANES), F32),
             ),
             in_specs=[anywhere(), anywhere(), anywhere(), vmem(), vmem(), vmem()],
             out_specs=(anywhere(), anywhere(), vmem(), vmem(), vmem(), vmem()),
@@ -894,13 +951,13 @@
                 pltpu.VMEM((vocab_loc, width), BF16),
                 pltpu.VMEM((toks, width), BF16),
                 pltpu.VMEM((steps, toks, VT), F32),
-                pltpu.VMEM((2, toks, 128), F32),
-                pltpu.VMEM((8, toks), F32),
-                pltpu.VMEM((NTP, 8, toks), F32),
-                pltpu.VMEM((8, toks), F32),
-                pltpu.VMEM((NY - 1, 8, toks), F32),
-                pltpu.VMEM((8, 128), F32),
-                pltpu.VMEM((NY - 1, 8, 128), F32),
+                pltpu.VMEM((2, toks, LANES), F32),
+                pltpu.VMEM((SUB, toks), F32),
+                pltpu.VMEM((NTP, SUB, toks), F32),
+                pltpu.VMEM((SUB, toks), F32),
+                pltpu.VMEM((NY - 1, SUB, toks), F32),
+                pltpu.VMEM((SUB, LANES), F32),
+                pltpu.VMEM((NY - 1, SUB, LANES), F32),
                 *tp_scratch,
                 dma(steps), pltpu.SemaphoreType.DMA, *twice(NTP), *twice(NY - 1), *twice(NY - 1), *tp_sems, *twice(sends), dma(2),
             ],
@@ -913,9 +970,9 @@
         lead = 16 * pl.cdiv(win, 48)
         middle = 2 * lead
         chunks = ((0, lead), (lead, middle), (middle, win))
-        third = 8 * pl.cdiv(win, 24)
+        third = SUB * pl.cdiv(win, 24)
         table_chunks = ((0, third), (third, 2 * third), (2 * third, win))
-        shares = SHARES if nz == 8 else (0.5,) * 3
+        shares = SHARES if nz == SUB else (0.5,) * 3
         table_parts = sum((two_colours(lo, hi, share) for (lo, hi), share in zip(table_chunks, shares)), [])
         table_plan = gather_plan((nz, NY), table_parts, 60)
         counts = [2 * len(p[0]) + 1 for p in (row_plan, dh_plan, table_plan)]
@@ -926,7 +983,7 @@
             ),
             out_shape=(
                 jax.ShapeDtypeStruct((toks, width), BF16),
-                jax.ShapeDtypeStruct((8, 128), F32),
+                jax.ShapeDtypeStruct((SUB, LANES), F32),
                 jax.ShapeDtypeStruct((nz, NY, win, cols), F32),
                 jax.ShapeDtypeStruct((NTP, NY, block, cols), F32),
             ),
@@ -934,7 +991,7 @@
             out_specs=(anywhere(), vmem(), anywhere(), anywhere()),
             scratch_shapes=[
                 *tp_scratch,
-                pltpu.VMEM((nz, NY, 8, 128), F32),
+                pltpu.VMEM((nz, NY, SUB, LANES), F32),
                 pltpu.VMEM((win, width), BF16),
                 pltpu.VMEM((NY * toks, width), BF16),
                 pltpu.VMEM((middle - lead, NY * toks), BF16),
@@ -951,8 +1008,8 @@
             compiler_params=pltpu.CompilerParams(collective_id=1, has_side_effects=True, vmem_limit_bytes=67_000_000),
             name="finish",
         )(table, ub.reshape(NY, toks, width), stats, grads, u_own, r_own, tiles)
-        depth = 16 if nz == 8 else 8
-        chunk = next(n for n in range(112, 0, -8) if stride % n == 0 and NY * stride >= n * depth)
+        depth = 16 if nz == SUB else SUB
+        chunk = next(n for n in range(112, 0, -SUB) if stride % n == 0 and NY * stride >= n * depth)
         d_table, d_rows, mean_loss = pl.pallas_call(
             functools.partial(place_kernel, chunk, tok_total),
             out_shape=(

time: 600 us -> 592 us (0.987)
  local copies, waits for them, and re-layouts: 18.1 us -> 1.01 us
  Pallas kernels: 577 us -> 586 us
    gather x1 -> x0, local copies, waits for them, and re-layouts: 17 us -> none  [per_device(): part = jnp.take(table, local_ids, axis=0, mode='clip')]
    pallas_call x0 -> x1, Pallas kernels: none -> 10.7 us  [per_device(): pl.pallas_call(pick_kernel, out_shape=jax.ShapeDtypeStruct((toks, width),...]
where the time goes in v4:
time: 592 us; the launch traced here: 591 us
  Pallas kernels  586 us (99%)
    pallas_call x1, Pallas kernels, per_device(): pl.pallas_call(functools.partial(finish_kernel, nz, stride, vocab_loc, to...  449 us
    pallas_call x1, Pallas kernels, per_device(): pl.pallas_call(functools.partial(token_kernel, nz, tok_total, token_plan)...  88.9 us
    pallas_call x1, Pallas kernels, per_device(): pl.pallas_call(functools.partial(place_kernel, chunk, tok_total), out_sha...  38.1 us

profile of v4, /device:TPU:1, one launch (start us, length us, event | category | flops | bytes accessed | tf_op | source)
XLA Modules:
  0.0 591.5 jit_solution(9134761086059638574)
XLA Ops:
  0.6 0.7 fusion.2
  1.3 0.1 select_n.30
  1.4 0.1 select_n.32
  1.5 0.7 pad_maximum_fusion.ids
  2.2 1.3 fusion.5
  3.5 0.6 fusion.1.group
  4.1 0.9 copy.9.marks
  5.0 10.7 %pick.1.part = bf16[512,2048]{1,0:T(8,128)(2,1)} custom-call(s32[512]{0:T(512)} %fusion.1.group, bf16[6288,2048]{1,0:T(8,128)(2,1)} %table.5, s32[512,2]{1,0:T(8,128)} %copy.9.marks), custom_call_target="tpu_custom_call" | custom-call | tf_op jit(solution)/shard_map/pick/pallas_call | solution.py:923
  15.7 88.9 %token_.1 = (bf16[13,512,512]{2,1,0:T(8,128)(2,1)}, f32[4,8,64,2048]{3,2,1,0:T(8,128)}, f32[64,2048]{1,0:T(8,128)}, f32[64,128]{1,0:T(8,128)}, f32[4,8,512]{2,1,0:T(8,128)}, /*index=5*/f32[4,8,128]{2,1,0:T(8,128)}) custom-call(bf16[6288,2048]{1,0:T(8,128)(2,1)} %table.5, bf16[512,2048]{1,0:T(8,128)(2,1)} %pick.1.part, bf16[512,2048]{1,0:T(8,128)(2,1)} %bitcast.9, ...), custom_call_target="tpu_custom_call" | custom-call | tf_op jit(solution)/shard_map/token/pallas_call | solution.py:935
  104.6 448.6 %finish.1 = (bf16[512,2048]{1,0:T(8,128)(2,1)}, f32[8,128]{1,0:T(8,128)}, f32[8,4,1584,256]{3,2,1,0:T(8,128)}, f32[8,4,512,256]{3,2,1,0:T(8,128)}) custom-call(bf16[6288,2048]{1,0:T(8,128)(2,1)} %table.5, f32[4,512,2048]{2,1,0:T(8,128)} %bitcast.8, f32[4,8,512]{2,1,0:T(8,128)} %get-tuple-element.16.stats, bf16[13,512,512]{2,1,0:T(8,128)(2,1)} %get-tuple-element.17.grads, ...), custom_call_target="tpu_custom_call" | custom-call | tf_op jit(solution)/shard_map/finish/pallas_call | solution.py:980
  553.2 38.1 %place.1 = (f32[6288,2048]{1,0:T(8,128)}, bf16[512,2048]{1,0:T(8,128)(2,1)}, f32[1,1]{1,0:T(1,128)}) custom-call(f32[8,4,1584,256]{3,2,1,0:T(8,128)} %get-tuple-element.21.stack, bf16[512,2048]{1,0:T(8,128)(2,1)} %get-tuple-element.22.rows_in, f32[8,128]{1,0:T(8,128)} %get-tuple-element.23.loss_in), custom_call_target="tpu_custom_call" | custom-call | tf_op jit(solution)/shard_map/place/pallas_call | solution.py:1013
  (1 shorter events, 0.0 us)

commit v5 on v4

--- a/solution.py
+++ b/solution.py
@@ -222,10 +222,14 @@
             self.forward(i).wait_send()
 
 
+def columns(row):
+    return jnp.transpose(jnp.broadcast_to(row.astype(F32), (LANES, row.shape[1]))).astype(jnp.int32)
+
+
 def token_kernel(
-    nz, tok_total, plan, table, part, trunk, marks, lab_row, ids,
+    nz, tok_total, plan, table, part, trunk, labels, ids,
     grads, ub_all, u_out, r_out, stats, tiles,
-    du, trunk_v, grad_v, table_v, ub_v, z_v, run, mine, theirs, row_out, row_in, tile_out, tile_in, pb, rl, fin, land,
+    lab_v, du, trunk_v, grad_v, table_v, ub_v, z_v, run, mine, theirs, row_out, row_in, tile_out, tile_in, pb, rl, fin, land,
     load_sem, part_sem, st_send, st_recv, row_send, row_recv, t_send, t_recv, rs_send, rs_recv, x_send, x_recv,
     grad_sem,
 ):
@@ -250,6 +254,7 @@
         table.at[pl.ds(whole * VT, tail)], table_v.at[pl.ds(whole * VT, tail)], load_sem.at[whole]
     )
     met_all = greet([to_tp(rem(at.tp + i, NTP)) for i in range(1, NTP)] + [to_dp(at.dp_of_y(i)) for i in range(1, NY)])
+    lab_v[ALL] = columns(labels[ALL]) - at.tp * rows
     part_copy.wait()
     for i in range(whole):
         load(i).start()
@@ -324,7 +329,7 @@
         z = jnp.where(lane >= i * VT - start, z, NEG)
         z_v[i] = z
         run[0] = jnp.maximum(run[0], fold(jnp.maximum, z))
-        hit = (lane + start == marks[:, 0:1]) & (lane >= i * VT - start)
+        hit = (lane + start == lab_v[:, 0:1]) & (lane >= i * VT - start)
         run[1] = run[1] + fold(jnp.add, jnp.where(hit, z, 0.0))
         return carry
 
@@ -357,9 +362,17 @@
     lse = peak + jnp.log(total)
     loss = jnp.sum(jnp.log(total) + peak - label, axis=1, keepdims=True)
     sub = lax.broadcasted_iota(jnp.int32, (SUB, toks), 0)
-    row_out[ALL] = jnp.where(sub == 0, lse, jnp.where(sub == 1, lab_row[ALL], 0.0))
-    upper = lax.broadcasted_iota(jnp.int32, ids.shape, 1) >= 64
-    tile_out[ALL] = jnp.where(upper == (rem(at.z, 2) == 1), ids[ALL], loss)
+    row_out[ALL] = jnp.where(sub == 0, lse, jnp.where(sub == 1, labels[ALL].astype(F32), 0.0))
+    odd = rem(at.z, 2) == 1
+    upper = lax.broadcasted_iota(jnp.int32, tile_out.shape, 1) >= 64
+    every = ids[ALL].astype(F32)
+    low = []
+    for j in range(0, toks, LANES):
+        pair = every[:, j : j + LANES]
+        low += [pair, jnp.concatenate([pair[:, 64:], pair[:, :64]], axis=1)]
+    low = jnp.concatenate(low, axis=0)
+    high = jnp.concatenate([low[:, 64:], low[:, :64]], axis=1)
+    tile_out[ALL] = jnp.where(upper == odd, jnp.where(odd, high, low), loss)
     tiles[0] = tile_out[ALL]
     rows_sent = []
     for i in range(NY - 1):
@@ -379,7 +392,7 @@
         start = start_of(i)
         shift = jnp.concatenate([run[0]] * (VT // LANES), axis=1)
         prob = jnp.exp(z_v[i] - shift)
-        hit = (lane + start == marks[:, 0:1]) & (lane >= i * VT - start)
+        hit = (lane + start == lab_v[:, 0:1]) & (lane >= i * VT - start)
 
         @pl.when(i >= 2)
         def _():
@@ -766,25 +779,28 @@
     blocks.end()
 
 
-def pick_kernel(group, table, marks, out, eights, sem):
+def pick_kernel(ids_s, table, ids, out, eights, local, sem):
     toks = out.shape[0]
     rows = table.shape[0]
+    begin = lax.axis_index("tp") * rows
     block = 32
 
     def fetch(t, carry):
-        eight = pl.multiple_of(group[t] * SUB, SUB)
+        row = ids_s[0, t] - begin
+        eight = pl.multiple_of(jnp.where((row >= 0) & (row < rows), lax.div(row, jnp.int32(SUB)), t) * SUB, SUB)
         mine = eights.at[pl.ds(pl.multiple_of(t * SUB, SUB), SUB)]
         pltpu.make_async_copy(table.at[pl.ds(eight, SUB)], mine, sem.at[lax.div(t, jnp.int32(part))]).start()
         return carry
 
     part = toks // sem.shape[0]
     lax.fori_loop(0, toks, fetch, 0, unroll=SUB)
+    local[ALL] = columns(ids[ALL]) - begin
     lane = lax.broadcasted_iota(jnp.int32, (block, SUB * block), 1)
     first = SUB * lax.broadcasted_iota(jnp.int32, (block, SUB * block), 0)
 
     def choose(b, carry):
         at = pl.multiple_of(b * block, block)
-        row = marks[pl.ds(at, block), 1:2]
+        row = local[pl.ds(at, block), 0:1]
         hit = (lane - first == rem(row, SUB)) & (row >= 0) & (row < rows)
         some = eights[pl.ds(pl.multiple_of(at * SUB, SUB), SUB * block), :]
         out[pl.ds(at, block)] = jnp.dot(
@@ -819,6 +835,16 @@
         s, row = rem(i, depth), pl.multiple_of(i * chunk, SUB)
         return pltpu.make_async_copy(slots.at[s], out.at[pl.ds(row, chunk)], store_sem.at[s])
 
+    rows_load = pltpu.make_async_copy(rows_in, rows_v, rows_sem)
+    rows_store = pltpu.make_async_copy(rows_v, rows_out, rows_sem)
+    used = per * chunk
+    left = have - used
+    rest = pltpu.make_async_copy(stack.at[:, ny - 1, pl.ds(used, left)], rest_v, rest_sem.at[0])
+    tails = [
+        pltpu.make_async_copy(rest_v.at[j], out.at[pl.ds(ny * used, left), pl.ds(j * cols, cols)], rest_sem.at[j])
+        for j in range(nz)
+    ]
+
     def prime(i, carry):
         for copy in loads(i):
             copy.start()
@@ -828,6 +854,14 @@
         for copy in loads(i):
             copy.wait()
         store(i).start()
+
+        @pl.when(i == ahead)
+        def _():
+            rows_load.wait()
+            rows_store.start()
+            rest.wait()
+            for copy in tails:
+                copy.start()
 
         @pl.when(i + ahead < total)
         def _():
@@ -844,25 +878,11 @@
         store(i).wait()
         return carry
 
-    rows_load = pltpu.make_async_copy(rows_in, rows_v, rows_sem)
-    rows_store = pltpu.make_async_copy(rows_v, rows_out, rows_sem)
     repeat(ahead, prime)
     rows_load.start()
-    used = per * chunk
-    left = have - used
-    rest = pltpu.make_async_copy(stack.at[:, ny - 1, pl.ds(used, left)], rest_v, rest_sem.at[0])
     rest.start()
-    tails = [
-        pltpu.make_async_copy(rest_v.at[j], out.at[pl.ds(ny * used, left), pl.ds(j * cols, cols)], rest_sem.at[j])
-        for j in range(nz)
-    ]
     lane = lax.broadcasted_iota(jnp.int32, (1, LANES), 1)
     loss_out[0, 0] = jnp.sum(jnp.where(rem(lane, 64) == 0, loss_in[0:1], 0.0)) / tok_total
-    rows_load.wait()
-    rows_store.start()
-    rest.wait()
-    for copy in tails:
-        copy.start()
     repeat(total, body)
     lax.fori_loop(total - 2 * ahead, total, drain, 0)
     for copy in tails:
@@ -901,11 +921,6 @@
         cols = width // nz
         block = nz * own
         big = 66_000_000
-        dp, tp = lax.axis_index("dp"), lax.axis_index("tp")
-        row_start = tp * vocab_loc
-        local_ids = ids.reshape(toks) - row_start
-        owned = (local_ids >= 0) & (local_ids < vocab_loc)
-
         tp_sems = twice(10)
         tp_scratch = [
             pltpu.VMEM((4, own, width), F32),
@@ -913,22 +928,16 @@
             pltpu.VMEM((4, own // 2, width), F32),
             pltpu.VMEM((NTP, own, width), F32),
         ]
-        ids_f = ids.reshape(NTP, own).astype(F32)
-        blank = jnp.zeros_like(ids_f)
-        even = rem(lax.div(dp, jnp.int32(NY)), 2) == 0
-        pad = ((0, 0), (0, LANES - 2 * own))
-        ids_tile = jnp.pad(jnp.concatenate([jnp.where(even, ids_f, blank), jnp.where(even, blank, ids_f)], axis=1), pad)
-        marks = jnp.stack([labels.reshape(toks) - row_start, local_ids], axis=1)
-        lab_row = labels.reshape(1, toks).astype(F32)
+        ids, labels = ids.reshape(1, toks), labels.reshape(1, toks)
         part = pl.pallas_call(
             pick_kernel,
             out_shape=jax.ShapeDtypeStruct((toks, width), BF16),
             in_specs=[pl.BlockSpec(memory_space=pltpu.SMEM), anywhere(), vmem()],
             out_specs=vmem(),
-            scratch_shapes=[pltpu.VMEM((SUB * toks, width), BF16), dma(SUB)],
+            scratch_shapes=[pltpu.VMEM((SUB * toks, width), BF16), pltpu.VMEM((toks, LANES), jnp.int32), dma(SUB)],
             compiler_params=pltpu.CompilerParams(vmem_limit_bytes=big),
             name="pick",
-        )(jnp.where(owned, local_ids // SUB, jnp.arange(toks)), table, marks)
+        )(ids, table, ids)
         steps = pl.cdiv(vocab_loc, VT)
         token_plan = gather_plan((NX, NY), two_colours(0, own, 0.5), 16, hold=2 * own)
         sends = 2 * len(token_plan[0]) + 1
@@ -942,9 +951,10 @@
                 jax.ShapeDtypeStruct((NY, SUB, toks), F32),
                 jax.ShapeDtypeStruct((NY, SUB, LANES), F32),
             ),
-            in_specs=[anywhere(), anywhere(), anywhere(), vmem(), vmem(), vmem()],
+            in_specs=[anywhere(), anywhere(), anywhere(), vmem(), vmem()],
             out_specs=(anywhere(), anywhere(), vmem(), vmem(), vmem(), vmem()),
             scratch_shapes=[
+                pltpu.VMEM((toks, LANES), jnp.int32),
                 pltpu.VMEM((toks, width), F32),
                 pltpu.VMEM((own, width), BF16),
                 pltpu.VMEM((2, toks, VT), BF16),
@@ -963,7 +973,7 @@
             ],
             compiler_params=pltpu.CompilerParams(collective_id=0, has_side_effects=True, vmem_limit_bytes=big),
             name="token",
-        )(table, part, trunk.reshape(toks, width), marks, lab_row, ids_tile)
+        )(table, part, trunk.reshape(toks, width), labels, ids)
 
         row_plan = gather_plan((NX, 1), two_colours(0, own, 1), 16)
         dh_plan = gather_plan((NX, NY), two_colours(0, block, 0.5), block // 4)

time: 592 us -> 587 us (level)
  no operation moved by 1% of the time
where the time goes in v5:
time: 587 us
  Pallas kernels  586 us (100%)
    pallas_call x1, Pallas kernels, per_device(): pl.pallas_call(functools.partial(finish_kernel, nz, stride, vocab_loc, to...  449 us
    pallas_call x1, Pallas kernels, per_device(): pl.pallas_call(functools.partial(token_kernel, nz, tok_total, token_plan)...  88.2 us
    pallas_call x1, Pallas kernels, per_device(): pl.pallas_call(functools.partial(place_kernel, chunk, tok_total), out_sha...  37 us
    pallas_call x1, Pallas kernels, per_device(): pl.pallas_call(pick_kernel, out_shape=jax.ShapeDtypeStruct((toks, width),...  12 us

profile of v5, /device:TPU:1, one launch (start us, length us, event | category | flops | bytes accessed | tf_op | source)
XLA Modules:
  0.0 586.7 jit_solution(5144512164226235352)
XLA Ops:
  0.6 12.0 %pick.1.part = bf16[512,2048]{1,0:T(8,128)(2,1)} custom-call(s32[1,512]{1,0:T(1,128)} %ids.3, bf16[6288,2048]{1,0:T(8,128)(2,1)} %table.5, s32[1,512]{1,0:T(1,128)} %ids.3), custom_call_target="tpu_custom_call" | custom-call | tf_op jit(solution)/shard_map/pick/pallas_call | solution.py:932
  12.7 88.2 %token_.1 = (bf16[13,512,512]{2,1,0:T(8,128)(2,1)}, f32[4,8,64,2048]{3,2,1,0:T(8,128)}, f32[64,2048]{1,0:T(8,128)}, f32[64,128]{1,0:T(8,128)}, f32[4,8,512]{2,1,0:T(8,128)}, /*index=5*/f32[4,8,128]{2,1,0:T(8,128)}) custom-call(bf16[6288,2048]{1,0:T(8,128)(2,1)} %table.5, bf16[512,2048]{1,0:T(8,128)(2,1)} %pick.1.part, bf16[512,2048]{1,0:T(8,128)(2,1)} %bitcast.5, ...), custom_call_target="tpu_custom_call" | custom-call | tf_op jit(solution)/shard_map/token/pallas_call | solution.py:944
  100.9 448.7 %finish.1 = (bf16[512,2048]{1,0:T(8,128)(2,1)}, f32[8,128]{1,0:T(8,128)}, f32[8,4,1584,256]{3,2,1,0:T(8,128)}, f32[8,4,512,256]{3,2,1,0:T(8,128)}) custom-call(bf16[6288,2048]{1,0:T(8,128)(2,1)} %table.5, f32[4,512,2048]{2,1,0:T(8,128)} %bitcast.4, f32[4,8,512]{2,1,0:T(8,128)} %get-tuple-element.16.stats, bf16[13,512,512]{2,1,0:T(8,128)(2,1)} %get-tuple-element.17.grads, ...), custom_call_target="tpu_custom_call" | custom-call | tf_op jit(solution)/shard_map/finish/pallas_call | solution.py:990
  549.5 37.0 %place.1 = (f32[6288,2048]{1,0:T(8,128)}, bf16[512,2048]{1,0:T(8,128)(2,1)}, f32[1,1]{1,0:T(1,128)}) custom-call(f32[8,4,1584,256]{3,2,1,0:T(8,128)} %get-tuple-element.21.stack, bf16[512,2048]{1,0:T(8,128)(2,1)} %get-tuple-element.22.rows_in, f32[8,128]{1,0:T(8,128)} %get-tuple-element.23.loss_in), custom_call_target="tpu_custom_call" | custom-call | tf_op jit(solution)/shard_map/place/pallas_call | solution.py:1023

commit v6 on v5

--- a/solution.py
+++ b/solution.py
@@ -14,6 +14,7 @@
 NY, NTP, NX = 4, 8, 4
 WAYS = (1, -1)
 SUB = 8
+AHEAD = 3
 LANES = 128
 BESIDE = ((0, 2, 1), (6, 1, 2), (13, 2, 2), (20, 1, 3), (26, 2, 3))
 SHARES = (0.55, 0.55, 0.7)
@@ -785,16 +786,25 @@
     begin = lax.axis_index("tp") * rows
     block = 32
 
-    def fetch(t, carry):
-        row = ids_s[0, t] - begin
-        eight = pl.multiple_of(jnp.where((row >= 0) & (row < rows), lax.div(row, jnp.int32(SUB)), t) * SUB, SUB)
-        mine = eights.at[pl.ds(pl.multiple_of(t * SUB, SUB), SUB)]
-        pltpu.make_async_copy(table.at[pl.ds(eight, SUB)], mine, sem.at[lax.div(t, jnp.int32(part))]).start()
-        return carry
-
-    part = toks // sem.shape[0]
-    lax.fori_loop(0, toks, fetch, 0, unroll=SUB)
+    parts = sem.shape[0]
+    part = toks // parts
+
+    def start(q):
+        def fetch(t, carry):
+            row = ids_s[0, t] - begin
+            spare = t * SUB
+            here = (row | (rows - 1 - row)) >= 0
+            eight = pl.multiple_of(jnp.where(here, row & -SUB, spare), SUB)
+            mine = eights.at[pl.ds(pl.multiple_of(spare, SUB), SUB)]
+            pltpu.make_async_copy(table.at[pl.ds(eight, SUB)], mine, sem.at[q]).start()
+            return carry
+
+        lax.fori_loop(q * part, (q + 1) * part, fetch, 0, unroll=2 * SUB)
+
+    start(0)
     local[ALL] = columns(ids[ALL]) - begin
+    for q in range(1, AHEAD):
+        start(q)
     lane = lax.broadcasted_iota(jnp.int32, (block, SUB * block), 1)
     first = SUB * lax.broadcasted_iota(jnp.int32, (block, SUB * block), 0)
 
@@ -808,7 +818,9 @@
         ).astype(BF16)
         return carry
 
-    for q in range(sem.shape[0]):
+    for q in range(parts):
+        if q + AHEAD < parts:
+            start(q + AHEAD)
         whole = pl.ds(q * part * SUB, part * SUB)
         pltpu.make_async_copy(table.at[pl.ds(0, part * SUB)], eights.at[whole], sem.at[q]).wait()
         lax.fori_loop(q * part // block, (q + 1) * part // block, choose, 0)

time: 587 us -> 585 us (level)
  no operation moved by 1% of the time
where the time goes in v6:
time: 585 us
  Pallas kernels  584 us (100%)
    pallas_call x1, Pallas kernels, per_device(): pl.pallas_call(functools.partial(finish_kernel, nz, stride, vocab_loc, to...  449 us
    pallas_call x1, Pallas kernels, per_device(): pl.pallas_call(functools.partial(token_kernel, nz, tok_total, token_plan)...  88.5 us
    pallas_call x1, Pallas kernels, per_device(): pl.pallas_call(functools.partial(place_kernel, chunk, tok_total), out_sha...  37 us

profile of v6, /device:TPU:1, one launch (start us, length us, event | category | flops | bytes accessed | tf_op | source)
XLA Modules:
  0.0 585.0 jit_solution(4423354215014969149)
XLA Ops:
  0.6 10.1 %pick.1.part = bf16[512,2048]{1,0:T(8,128)(2,1)} custom-call(s32[1,512]{1,0:T(1,128)} %ids.3, bf16[6288,2048]{1,0:T(8,128)(2,1)} %table.5, s32[1,512]{1,0:T(1,128)} %ids.3), custom_call_target="tpu_custom_call" | custom-call | tf_op jit(solution)/shard_map/pick/pallas_call | solution.py:944
  10.8 88.5 %token_.1 = (bf16[13,512,512]{2,1,0:T(8,128)(2,1)}, f32[4,8,64,2048]{3,2,1,0:T(8,128)}, f32[64,2048]{1,0:T(8,128)}, f32[64,128]{1,0:T(8,128)}, f32[4,8,512]{2,1,0:T(8,128)}, /*index=5*/f32[4,8,128]{2,1,0:T(8,128)}) custom-call(bf16[6288,2048]{1,0:T(8,128)(2,1)} %table.5, bf16[512,2048]{1,0:T(8,128)(2,1)} %pick.1.part, bf16[512,2048]{1,0:T(8,128)(2,1)} %bitcast.5, ...), custom_call_target="tpu_custom_call" | custom-call | tf_op jit(solution)/shard_map/token/pallas_call | solution.py:956
  99.3 448.5 %finish.1 = (bf16[512,2048]{1,0:T(8,128)(2,1)}, f32[8,128]{1,0:T(8,128)}, f32[8,4,1584,256]{3,2,1,0:T(8,128)}, f32[8,4,512,256]{3,2,1,0:T(8,128)}) custom-call(bf16[6288,2048]{1,0:T(8,128)(2,1)} %table.5, f32[4,512,2048]{2,1,0:T(8,128)} %bitcast.4, f32[4,8,512]{2,1,0:T(8,128)} %get-tuple-element.16.stats, bf16[13,512,512]{2,1,0:T(8,128)(2,1)} %get-tuple-element.17.grads, ...), custom_call_target="tpu_custom_call" | custom-call | tf_op jit(solution)/shard_map/finish/pallas_call | solution.py:1002
  547.8 37.0 %place.1 = (f32[6288,2048]{1,0:T(8,128)}, bf16[512,2048]{1,0:T(8,128)(2,1)}, f32[1,1]{1,0:T(1,128)}) custom-call(f32[8,4,1584,256]{3,2,1,0:T(8,128)} %get-tuple-element.21.stack, bf16[512,2048]{1,0:T(8,128)(2,1)} %get-tuple-element.22.rows_in, f32[8,128]{1,0:T(8,128)} %get-tuple-element.23.loss_in), custom_call_target="tpu_custom_call" | custom-call | tf_op jit(solution)/shard_map/place/pallas_call | solution.py:1035
